TPU v7x, 32 devices: a 4x2x2 block of a 4x4x8 slice. The times are simulated.
32 devices in a mesh: dp: 4 (over y, z), tp: 8 (over x, core).
Axes of the slice: x: 4, y: 2, z: 2, core: 2. Of those that a mesh axis runs over, the one named last changes fastest.
The devices are a block of a 4x4x8 slice.
Arguments:
- x_in: bfloat16 [32, 256, 4096], P('dp'), parts along dimension 0
- adapter_ids: int32 [32], P('dp'), parts along dimension 0
- gain_attn: float32 [4096], replicated
- gain_mlp: float32 [4096], replicated
- w_q: bfloat16 [4096, 32, 128], P(None, 'tp')
- w_k: bfloat16 [4096, 8, 128], P(None, 'tp')
- w_v: bfloat16 [4096, 8, 128], P(None, 'tp')
- w_o: bfloat16 [32, 128, 4096], P('tp')
- w_gate: bfloat16 [4096, 14336], P(None, 'tp')
- w_up: bfloat16 [4096, 14336], P(None, 'tp')
- w_down: bfloat16 [14336, 4096], P('tp')
- a_q: bfloat16 [8, 4096, 8], P(None, None, 'tp')
- b_q: bfloat16 [8, 8, 32, 128], P(None, None, 'tp')
- a_k: bfloat16 [8, 4096, 8], P(None, None, 'tp')
- b_k: bfloat16 [8, 8, 8, 128], P(None, None, 'tp')
- a_v: bfloat16 [8, 4096, 8], P(None, None, 'tp')
- b_v: bfloat16 [8, 8, 8, 128], P(None, None, 'tp')
- a_o: bfloat16 [8, 32, 128, 8], P(None, 'tp')
- b_o: bfloat16 [8, 8, 4096], P(None, None, 'tp')
- a_gate: bfloat16 [8, 4096, 8], P(None, None, 'tp')
- b_gate: bfloat16 [8, 8, 14336], P(None, None, 'tp')
- a_up: bfloat16 [8, 4096, 8], P(None, None, 'tp')
- b_up: bfloat16 [8, 8, 14336], P(None, None, 'tp')
- a_down: bfloat16 [8, 14336, 8], P(None, 'tp')
- b_down: bfloat16 [8, 8, 4096], P(None, None, 'tp')
Outputs:
- output: bfloat16 [32, 256, 4096], P('dp'), parts along dimension 0
There are 4 independent parts. A program takes and returns all parts, laid end to end along the dimension named above; an argument that names none is the same for every part.
All inputs are finite; a program needn't handle non-finite values.
Results may differ from a plain program's by a relative error of at most 0.02.
Values are sent between devices in bfloat16 or wider.
A program may use at most 768 MiB of HBM per device.

v0:
```python
import jax
import jax.numpy as jnp
from jax import lax
from jax.sharding import PartitionSpec as P

value_a10 = 16
RMS_EPS = 1e-5


def rms_scale(x_in, gain_vec):
    x_f32 = x_in.astype(jnp.float32)
    inv_rms = lax.rsqrt(jnp.mean(x_f32 * x_f32, axis=-1, keepdims=True) + RMS_EPS)
    return (x_f32 * inv_rms * gain_vec).astype(jnp.bfloat16)


def causal_attention(q_flat, k_flat, v_flat, kv_heads, head_dim):
    num_seqs, seq_len = q_flat.shape[0], q_flat.shape[1]
    q_group = q_flat.reshape(num_seqs, seq_len, kv_heads, -1, head_dim)
    k_group = k_flat.reshape(num_seqs, seq_len, kv_heads, head_dim)
    v_group = v_flat.reshape(num_seqs, seq_len, kv_heads, head_dim)
    scores = jnp.einsum('bqngd,bknd->bngqk', q_group, k_group, preferred_element_type=jnp.float32) * head_dim ** -0.5
    causal = jnp.arange(seq_len)[:, None] >= jnp.arange(seq_len)[None, :]
    prob_bf = jax.nn.softmax(jnp.where(causal, scores, -jnp.inf), axis=-1).astype(jnp.bfloat16)
    att_out = jnp.einsum('bngqk,bknd->bqngd', prob_bf, v_group, preferred_element_type=jnp.float32)
    return att_out.astype(jnp.bfloat16).reshape(num_seqs, seq_len, -1)


def column_proj(h_in, w_loc, a_sel, b_sel, scale):
    value_a9 = jnp.einsum('bsd,bdr->bsr', h_in, a_sel, preferred_element_type=jnp.float32).astype(jnp.bfloat16)
    value_a8 = lax.all_gather(value_a9, 'tp', axis=2, tiled=True)
    base_out = jnp.einsum('bsd,de->bse', h_in, w_loc, preferred_element_type=jnp.float32)
    array_b8 = jnp.einsum('bsr,bre->bse', value_a8, b_sel, preferred_element_type=jnp.float32)
    return (base_out + scale * array_b8).astype(jnp.bfloat16)


def row_proj(h_in, w_loc, a_sel, b_sel, scale, resid_full):
    base_part = jnp.einsum('bse,ed->bsd', h_in, w_loc, preferred_element_type=jnp.float32).astype(jnp.bfloat16)
    value_a9 = jnp.einsum('bse,ber->bsr', h_in, a_sel, preferred_element_type=jnp.float32).astype(jnp.bfloat16)
    base_sum = lax.psum_scatter(base_part, 'tp', scatter_dimension=2, tiled=True)
    value_a8 = lax.psum(value_a9, 'tp')
    width = base_sum.shape[2]
    resid_loc = lax.dynamic_slice_in_dim(resid_full, lax.axis_index('tp') * width, width, axis=2)
    array_b8 = jnp.einsum('bsr,brd->bsd', value_a8, b_sel, preferred_element_type=jnp.float32)
    out_loc = resid_loc.astype(jnp.float32) + base_sum.astype(jnp.float32) + scale * array_b8
    return lax.all_gather(out_loc.astype(jnp.bfloat16), 'tp', axis=2, tiled=True)


def solution(mesh):
    act_spec = P('dp', None, None)
    w_head_spec = P(None, 'tp', None)
    w_out_spec = P('tp', None, None)
    w_col_spec = P(None, 'tp')
    w_row_spec = P('tp', None)
    a_rank_spec = P(None, None, 'tp')
    b_head_spec = P(None, None, 'tp', None)
    b_col_spec = P(None, None, 'tp')
    a_head_spec = P(None, 'tp', None, None)
    a_row_spec = P(None, 'tp', None)
    in_specs = (act_spec, P('dp'), P(None), P(None), w_head_spec, w_head_spec, w_head_spec, w_out_spec,
                w_col_spec, w_col_spec, w_row_spec, a_rank_spec, b_head_spec, a_rank_spec, b_head_spec,
                a_rank_spec, b_head_spec, a_head_spec, b_col_spec, a_rank_spec, b_col_spec,
                a_rank_spec, b_col_spec, a_row_spec, b_col_spec)

    def local_layer(x_in, adapter_ids, gain_attn, gain_mlp, w_q, w_k, w_v, w_o, w_gate, w_up, w_down,
                    a_q, b_q, a_k, b_k, a_v, b_v, a_o, b_o, a_gate, b_gate, a_up, b_up, a_down, b_down):
        num_seqs, model_dim = x_in.shape[0], x_in.shape[2]
        rank = b_q.shape[1]
        scale = value_a10 / rank

        def per_sequence(stack):
            return jnp.take(stack, adapter_ids, axis=0)

        def column(h_in, w_loc, a_stack, b_stack):
            return column_proj(h_in, w_loc.reshape(model_dim, -1), per_sequence(a_stack),
                               per_sequence(b_stack).reshape(num_seqs, rank, -1), scale)

        h_norm = rms_scale(x_in, gain_attn)
        q_loc = column(h_norm, w_q, a_q, b_q)
        k_loc = column(h_norm, w_k, a_k, b_k)
        v_loc = column(h_norm, w_v, a_v, b_v)
        att_loc = causal_attention(q_loc, k_loc, v_loc, w_k.shape[1], w_k.shape[2])
        x_one = row_proj(att_loc, w_o.reshape(-1, model_dim), per_sequence(a_o).reshape(num_seqs, -1, rank),
                         per_sequence(b_o), scale, x_in)
        h_two = rms_scale(x_one, gain_mlp)
        gate_loc = column(h_two, w_gate, a_gate, b_gate)
        up_loc = column(h_two, w_up, a_up, b_up)
        mlp_mid = (jax.nn.silu(gate_loc.astype(jnp.float32)) * up_loc.astype(jnp.float32)).astype(jnp.bfloat16)
        return row_proj(mlp_mid, w_down, per_sequence(a_down), per_sequence(b_down), scale, x_one)

    return jax.shard_map(local_layer, mesh=mesh, in_specs=in_specs, out_specs=act_spec, check_vma=False)
```

profile of v0, /device:TPU:81, one launch (start us, length us, event | category | flops | bytes accessed | tf_op | source)
XLA Modules:
  0.0 739.4 jit_solution(16795611578601501544)
XLA Ops:
  15.6 7.5 %fusion = f32[8,256]{1,0:T(8,128)S(1)} fusion(bf16[8,256,4096]{2,1,0:T(8,128)(2,1)} %param.33), kind=kLoop, calls=%fused_computation.18 | loop fusion | flops 25163776 | bytes 16785408 | tf_op jit(solution)/shard_map/reduce_sum | solution.py:12
  30.9 15.1 %all_gather.23 = bf16[8,256,8]{1,0,2:T(8,128)(2,1)S(1)} all-gather(bf16[8,256,1]{1,0,2:T(8,128)(2,1)S(1)} %bitcast.172), channel_id=1, replica_groups=mesh['dp'=4,'tp'=8] {'tp'}, dimensions={2}, use_global_device_ids=true | all-gather | bytes 36864 | tf_op jit(solution)/shard_map/all_gather | solution.py:30
  53.8 15.0 %fusion.119 = f32[8,256,512]{2,1,0:T(8,128)} fusion(bf16[4096,512,1]{1,0,2:T(8,128)(2,1)} %reshape.355, bf16[8,256,4096]{2,1,0:T(8,128)(2,1)} %param.33, f32[4096]{0:T(1024)S(1)} %copy-done.19, f32[8,256]{1,0:T(8,128)S(1)} %add_rsqrt_fusion.1), kind=kOutput, calls=%fused_computation.152 | convolution fusion | flops 8623489024 | bytes 25190400 | tf_op jit(solution)/shard_map/bsd,de->bse/dot_general | solution.py:31
  68.8 8.1 %fusion.61 = bf16[8,1,256]{2,1,0:T(2,128)(2,1)S(1)} fusion(bf16[8,4096,1]{1,0,2:T(8,128)(2,1)S(1)} %get-tuple-element.8, bf16[8,256,4096]{2,1,0:T(8,128)(2,1)} %param.33, f32[4096]{0:T(1024)S(1)} %copy-done.19, f32[8,256]{1,0:T(8,128)S(1)} %add_rsqrt_fusion.1), kind=kOutput, calls=%fused_computation.87 | convolution fusion | flops 50331648 | bytes 16871424 | tf_op jit(solution)/shard_map/bsd,bdr->bsr/dot_general | solution.py:29
  77.0 13.5 %all_gather.22 = bf16[8,256,8]{1,0,2:T(8,128)(2,1)S(1)} all-gather(bf16[8,256,1]{1,0,2:T(8,128)(2,1)S(1)} %bitcast.173), channel_id=1, replica_groups=mesh['dp'=4,'tp'=8] {'tp'}, dimensions={2}, use_global_device_ids=true | all-gather | bytes 36864 | tf_op jit(solution)/shard_map/all_gather | solution.py:30
  91.0 11.4 %fusion.44 = f32[8,256,128]{2,1,0:T(8,128)} fusion(bf16[4096,1,128]{2,0,1:T(8,128)(2,1)S(1)} %copy-done, bf16[8,256,4096]{2,1,0:T(8,128)(2,1)} %param.33, f32[4096]{0:T(1024)S(1)} %copy-done.19, f32[8,256]{1,0:T(8,128)S(1)} %add_rsqrt_fusion.1), kind=kOutput, calls=%fused_computation.69 | convolution fusion | flops 2181038080 | bytes 18898944 | tf_op jit(solution)/shard_map/bsd,de->bse/dot_general | solution.py:31
  102.5 8.2 %fusion.63 = bf16[8,1,256]{2,1,0:T(2,128)(2,1)S(1)} fusion(bf16[8,4096,1]{1,0,2:T(8,128)(2,1)S(1)} %get-tuple-element.13, bf16[8,256,4096]{2,1,0:T(8,128)(2,1)} %param.33, f32[4096]{0:T(1024)S(1)} %copy-done.19, f32[8,256]{1,0:T(8,128)S(1)} %add_rsqrt_fusion.1), kind=kOutput, calls=%fused_computation.89 | convolution fusion | flops 50331648 | bytes 16871424 | tf_op jit(solution)/shard_map/bsd,bdr->bsr/dot_general | solution.py:29
  110.7 13.1 %all_gather.21 = bf16[8,256,8]{1,0,2:T(8,128)(2,1)S(1)} all-gather(bf16[8,256,1]{1,0,2:T(8,128)(2,1)S(1)} %bitcast.174), channel_id=1, replica_groups=mesh['dp'=4,'tp'=8] {'tp'}, dimensions={2}, use_global_device_ids=true | all-gather | bytes 36864 | tf_op jit(solution)/shard_map/all_gather | solution.py:30
  124.4 11.6 %fusion.46 = f32[8,256,128]{2,1,0:T(8,128)} fusion(bf16[4096,1,128]{2,0,1:T(8,128)(2,1)S(1)} %copy-done.18, bf16[8,256,4096]{2,1,0:T(8,128)(2,1)} %param.33, f32[4096]{0:T(1024)S(1)} %copy-done.19, f32[8,256]{1,0:T(8,128)S(1)} %add_rsqrt_fusion.1), kind=kOutput, calls=%fused_computation.71 | convolution fusion | flops 2181038080 | bytes 18898944 | tf_op jit(solution)/shard_map/bsd,de->bse/dot_general | solution.py:31
  152.8 14.8 %convolution_convert_fusion = bf16[8,256,4096]{2,1,0:T(8,128)(2,1)} fusion(bf16[8,256,512]{1,2,0:T(8,128)(2,1)S(1)} %bitcast.170, bf16[512,4096,1]{1,0,2:T(8,128)(2,1)} %bitcast.179), kind=kOutput, calls=%fused_computation.39 | convolution fusion | flops 8598323200 | bytes 23068672 | tf_op jit(solution)/shard_map/bse,ed->bsd/dot_general | solution.py:37
  170.0 22.7 %psum.14 = bf16[8,256,8]{1,2,0:T(8,128)(2,1)S(1)} all-reduce(bf16[8,256,8]{1,2,0:T(8,128)(2,1)S(1)} %convolution_convert_fusion.2), channel_id=1, replica_groups=mesh['dp'=4,'tp'=8] {'tp'}, use_global_device_ids=true, to_apply=%region_4.7 | all-reduce | flops 16384 | bytes 65536 | tf_op jit(solution)/shard_map/psum | solution.py:40
  192.7 65.6 %reduce-scatter.3.cloned.1.call-done = bf16[8,256,512]{2,1,0:T(8,128)(2,1)} async-done(((bf16[8,256,4096]{2,1,0:T(8,128)(2,1)}), bf16[8,256,512]{2,1,0:T(8,128)(2,1)}) %reduce-scatter.3.cloned.1.call-update) | async-done | bytes 2097168 | tf_op jit(solution)/shard_map/reduce_scatter | solution.py:39
  264.2 81.5 %all-gather.3.cloned.1.call-done = bf16[8,256,4096]{2,1,0:T(8,128)(2,1)} async-done(((bf16[8,256,512]{2,1,0:T(8,128)(2,1)}), bf16[8,256,4096]{2,1,0:T(8,128)(2,1)}) %all-gather.3.cloned.1.call-update) | async-done | bytes 16777232 | tf_op jit(solution)/shard_map/all_gather | solution.py:45
  345.7 8.0 %fusion.3 = f32[8,256]{1,0:T(8,128)S(1)} fusion(bf16[8,256,4096]{2,1,0:T(8,128)(2,1)} %all-gather.3.cloned.1.call-done), kind=kLoop, calls=%fused_computation.21 | loop fusion | flops 25163776 | bytes 16785408 | tf_op jit(solution)/shard_map/reduce_sum | solution.py:12
  361.0 13.0 %all_gather.26 = bf16[8,256,8]{1,0,2:T(8,128)(2,1)S(1)} all-gather(bf16[8,256,1]{1,0,2:T(8,128)(2,1)S(1)} %bitcast.175), channel_id=1, replica_groups=mesh['dp'=4,'tp'=8] {'tp'}, dimensions={2}, use_global_device_ids=true | all-gather | bytes 36864 | tf_op jit(solution)/shard_map/all_gather | solution.py:30
  378.7 12.9 %all_gather.25 = bf16[8,256,8]{1,0,2:T(8,128)(2,1)S(1)} all-gather(bf16[8,256,1]{1,0,2:T(8,128)(2,1)S(1)} %bitcast.176), channel_id=1, replica_groups=mesh['dp'=4,'tp'=8] {'tp'}, dimensions={2}, use_global_device_ids=true | all-gather | bytes 36864 | tf_op jit(solution)/shard_map/all_gather | solution.py:30
  398.9 43.8 %fusion.12 = f32[8,256,1792]{2,1,0:T(8,128)} fusion(bf16[4096,1792]{1,0:T(8,128)(2,1)} %param.42, bf16[8,256,4096]{2,1,0:T(8,128)(2,1)S(1)} %copy-done.4, f32[4096]{0:T(1024)S(1)} %copy-done.20, f32[8,256]{1,0:T(8,128)S(1)} %add_rsqrt_fusion), kind=kOutput, calls=%fused_computation.32 | convolution fusion | flops 30098325504 | bytes 46161920 | tf_op jit(solution)/shard_map/bsd,de->bse/dot_general | solution.py:31
  442.7 43.6 %fusion.14 = f32[8,256,1792]{2,1,0:T(8,128)} fusion(bf16[4096,1792]{1,0:T(8,128)(2,1)} %param.41, bf16[8,256,4096]{2,1,0:T(8,128)(2,1)S(1)} %copy-done.4, f32[4096]{0:T(1024)S(1)} %copy-done.20, f32[8,256]{1,0:T(8,128)S(1)} %add_rsqrt_fusion), kind=kOutput, calls=%fused_computation.34 | convolution fusion | flops 30098325504 | bytes 46161920 | tf_op jit(solution)/shard_map/bsd,de->bse/dot_general | solution.py:31
  486.3 19.5 %fusion.16 = bf16[8,256,1792]{2,1,0:T(8,128)(2,1)} fusion(f32[8,256,1792]{2,1,0:T(8,128)} %fusion.14, f32[8,256,1792]{2,1,0:T(8,128)} %fusion.51, f32[8,256,1792]{2,1,0:T(8,128)} %fusion.12, bf16[8,8,1792]{2,1,0:T(8,128)(2,1)S(1)} %gather_fusion.12, pred[8]{0:T(512)(128)(4,1)S(1)} %compare_and_fusion, bf16[8,256,8]{1,0,2:T(8,128)(2,1)S(1)} %all_gather.26), kind=kOutput, calls=%fused_computation.38 | convolution fusion | flops 110215168 | bytes 51642376 | tf_op jit(solution)/shard_map/bsr,bre->bse/dot_general | solution.py:32
  505.8 37.5 %fusion.17 = bf16[8,256,4096]{2,1,0:T(8,128)(2,1)} fusion(bf16[8,256,1792]{2,1,0:T(8,128)(2,1)} %fusion.16, bf16[1792,4096]{1,0:T(8,128)(2,1)} %param.43), kind=kOutput, calls=%fused_computation.40 | convolution fusion | flops 30073159680 | bytes 38797312 | tf_op jit(solution)/shard_map/bse,ed->bsd/dot_general | solution.py:37
  550.7 21.5 %psum.15 = bf16[8,256,8]{1,2,0:T(8,128)(2,1)S(1)} all-reduce(bf16[8,256,8]{1,2,0:T(8,128)(2,1)S(1)} %convolution_convert_fusion.1), channel_id=1, replica_groups=mesh['dp'=4,'tp'=8] {'tp'}, use_global_device_ids=true, to_apply=%region_7.12 | all-reduce | flops 16384 | bytes 65536 | tf_op jit(solution)/shard_map/psum | solution.py:40
  572.1 59.1 %reduce-scatter.5.cloned.1.call-done = bf16[8,256,512]{2,1,0:T(8,128)(2,1)} async-done(((bf16[8,256,4096]{2,1,0:T(8,128)(2,1)}), bf16[8,256,512]{2,1,0:T(8,128)(2,1)}) %reduce-scatter.5.cloned.1.call-update) | async-done | bytes 2097168 | tf_op jit(solution)/shard_map/reduce_scatter | solution.py:39
  635.8 82.7 %all-gather.5.cloned.1.call-done = bf16[8,256,4096]{2,1,0:T(8,128)(2,1)} async-done(((bf16[8,256,512]{2,1,0:T(8,128)(2,1)}), bf16[8,256,4096]{2,1,0:T(8,128)(2,1)}) %all-gather.5.cloned.1.call-update) | async-done | bytes 16777232 | tf_op jit(solution)/shard_map/all_gather | solution.py:45
  718.6 14.1 %copy.116 = bf16[8,256,4096]{2,1,0:T(8,128)(2,1)} copy(bf16[8,256,4096]{2,1,0:T(8,128)(2,1)} %all-gather.5.cloned.1.call-done) | data formatting | bytes 33554432
  (90 shorter events, 81.9 us)
Async XLA Ops:
  6.5 84.5 %copy-start = (bf16[4096,1,128]{2,0,1:T(8,128)(2,1)S(1)}, bf16[4096,1,128]{2,0,1:T(8,128)(2,1)}, u32[]{:S(2)}) copy-start(bf16[4096,1,128]{2,0,1:T(8,128)(2,1)} %param.38) | copy-start | bytes 3145732
  6.6 17.2 %copy-start.19 = (f32[4096]{0:T(1024)S(1)}, f32[4096]{0:T(1024)}, u32[]{:S(2)}) copy-start(f32[4096]{0:T(1024)} %param.35) | copy-start | bytes 49156
  6.6 251.8 %reduce-scatter.3.cloned.1.call-start = ((), (), s32[]{:S(2)}) async-start(), calls=%async_computation.2 | async-start | bytes 18874368 | tf_op jit(solution)/shard_map/reduce_scatter | solution.py:39
  8.0 255.6 %copy-start.15 = (s32[1024]{0:T(1024)}, s32[1024]{0:T(1024)S(1)}, u32[]{:S(2)}) copy-start(s32[1024]{0:T(1024)S(1)} %pad_clamp_fusion) | copy-start | bytes 12292
  15.6 10.7 %copy-start.3 = (bf16[8,256,4096]{2,1,0:T(8,128)(2,1)S(1)}, bf16[8,256,4096]{2,1,0:T(8,128)(2,1)}, u32[]{:S(2)}) copy-start(bf16[8,256,4096]{2,1,0:T(8,128)(2,1)} %param.33) | copy-start | bytes 50331652
  26.3 19.7 %copy-start.12 = (bf16[8,8,4,128]{3,2,1,0:T(4,128)(2,1)S(1)}, bf16[8,8,4,128]{3,2,1,0:T(4,128)(2,1)}, u32[]{:S(2)}) copy-start(bf16[8,8,4,128]{3,2,1,0:T(4,128)(2,1)} %param.45) | copy-start | bytes 196612
  68.8 21.6 %copy-start.16 = (bf16[8,8,1,128]{3,1,2,0:T(8,128)(2,1)S(1)}, bf16[8,8,1,128]{3,1,2,0:T(8,128)(2,1)}, u32[]{:S(2)}) copy-start(bf16[8,8,1,128]{3,1,2,0:T(8,128)(2,1)} %param.47) | copy-start | bytes 49156
  102.5 21.4 %copy-start.17 = (bf16[8,8,1,128]{3,1,2,0:T(8,128)(2,1)S(1)}, bf16[8,8,1,128]{3,1,2,0:T(8,128)(2,1)}, u32[]{:S(2)}) copy-start(bf16[8,8,1,128]{3,1,2,0:T(8,128)(2,1)} %param.49) | copy-start | bytes 49156
  102.5 21.9 %copy-start.18 = (bf16[4096,1,128]{2,0,1:T(8,128)(2,1)S(1)}, bf16[4096,1,128]{2,0,1:T(8,128)(2,1)}, u32[]{:S(2)}) copy-start(bf16[4096,1,128]{2,0,1:T(8,128)(2,1)} %param.39) | copy-start | bytes 3145732
  124.4 11.6 %copy-start.6 = (f32[8,256,512]{2,1,0:T(8,128)S(1)}, f32[8,256,512]{2,1,0:T(8,128)}, u32[]{:S(2)}) copy-start(f32[8,256,512]{2,1,0:T(8,128)} %fusion.119) | copy-start | bytes 12582916
  124.4 12.4 %copy-start.7 = (f32[8,256,128]{2,1,0:T(8,128)S(1)}, f32[8,256,128]{2,1,0:T(8,128)}, u32[]{:S(2)}) copy-start(f32[8,256,128]{2,1,0:T(8,128)} %fusion.44) | copy-start | bytes 3145732
  167.6 1.4 copy-start.13
  167.6 95.4 %copy-start.8 = (bf16[8,8,1792]{2,1,0:T(8,128)(2,1)S(1)}, bf16[8,8,1792]{2,1,0:T(8,128)(2,1)}, u32[]{:S(2)}) copy-start(bf16[8,8,1792]{2,1,0:T(8,128)(2,1)} %param.53) | copy-start | bytes 688132
  167.6 96.0 %copy-start.9 = (bf16[8,8,1792]{2,1,0:T(8,128)(2,1)S(1)}, bf16[8,8,1792]{2,1,0:T(8,128)(2,1)}, u32[]{:S(2)}) copy-start(bf16[8,8,1792]{2,1,0:T(8,128)(2,1)} %param.55) | copy-start | bytes 688132
  167.6 178.1 %all-gather.3.cloned.1.call-start = ((), (), s32[]{:S(2)}) async-start(), calls=%async_computation.3 | async-start | bytes 18874368 | tf_op jit(solution)/shard_map/all_gather | solution.py:45
  169.0 184.7 %copy-start.11 = (bf16[8,4096,1]{1,0,2:T(8,128)(2,1)S(1)}, bf16[8,4096,1]{1,0,2:T(8,128)(2,1)}, u32[]{:S(2)}) copy-start(bf16[8,4096,1]{1,0,2:T(8,128)(2,1)} %get-tuple-element.6) | copy-start | bytes 196612
  169.0 184.7 %copy-start.20 = (f32[4096]{0:T(1024)S(1)}, f32[4096]{0:T(1024)}, u32[]{:S(2)}) copy-start(f32[4096]{0:T(1024)} %param.36) | copy-start | bytes 49156
  262.9 368.3 %reduce-scatter.5.cloned.1.call-start = ((), (), s32[]{:S(2)}) async-start(), calls=%async_computation.4 | async-start | bytes 18874368 | tf_op jit(solution)/shard_map/reduce_scatter | solution.py:39
  345.7 10.7 %copy-start.4 = (bf16[8,256,4096]{2,1,0:T(8,128)(2,1)S(1)}, bf16[8,256,4096]{2,1,0:T(8,128)(2,1)}, u32[]{:S(2)}) copy-start(bf16[8,256,4096]{2,1,0:T(8,128)(2,1)} %all-gather.3.cloned.1.call-done) | copy-start | bytes 50331652
  356.3 17.7 %copy-start.10 = (bf16[8,4096,1]{1,0,2:T(8,128)(2,1)S(1)}, bf16[8,4096,1]{1,0,2:T(8,128)(2,1)}, u32[]{:S(2)}) copy-start(bf16[8,4096,1]{1,0,2:T(8,128)(2,1)} %get-tuple-element.12) | copy-start | bytes 196612
  543.3 0.9 copy-start.2
  543.3 1.6 copy-start.14
  543.3 175.2 %all-gather.5.cloned.1.call-start = ((), (), s32[]{:S(2)}) async-start(), calls=%async_computation.5 | async-start | bytes 18874368 | tf_op jit(solution)/shard_map/all_gather | solution.py:45
  635.8 96.8 %copy-start.1 = (bf16[4096,1,128]{2,0,1:T(8,128)(2,1)S(1)}, bf16[4096,1,128]{2,0,1:T(8,128)(2,1)}, u32[]{:S(2)}) copy-start(bf16[4096,1,128]{2,0,1:T(8,128)(2,1)} %param.38) | copy-start | bytes 3145732
  (1 other events, 0.8 us)
Sparse Core Ops, SparseCore 0:
  167.8 90.5 reduce-scatter.2
  263.0 82.5 all-gather.2
  543.5 87.7 reduce-scatter.4
  636.0 82.5 all-gather.4
where the time goes:
time: 745 us; the launch traced here: 739 us
  waiting for transfers between devices  289 us (39%)
  matrix products  261 us (35%)
  blocking collectives  112 us (15%)
  local copies, waits for them, and re-layouts  40.8 us (5%)
  other arithmetic  22.8 us (3%)
  between operations  13.7 us (2%)
    all_gather x2, waiting for transfers between devices, row_proj(): lax.all_gather(out_loc.astype(jnp.bfloat16), 'tp', axis=2, tiled=True)  164 us
    dot_general x5, matrix products, column_proj(): jnp.einsum('bsd,de->bse', h_in, w_loc, preferred_element_type=jnp.float32)  125 us
    reduce_scatter x2, waiting for transfers between devices, row_proj(): lax.psum_scatter(base_part, 'tp', scatter_dimension=2, tiled=True)  125 us
    all_gather x5, blocking collectives, column_proj(): value_a8 = lax.all_gather(value_a9, 'tp', axis=2, tiled=True)  67.6 us
    dot_general x2, matrix products, row_proj(): jnp.einsum('bse,ed->bsd', h_in, w_loc, preferred_element_type=jnp.float32)  52.2 us
    psum x2, blocking collectives, row_proj(): value_a8 = lax.psum(value_a9, 'tp')  44.2 us
    dot_general x5, matrix products, column_proj(): jnp.einsum('bsd,bdr->bsr', h_in, a_sel, preferred_element_type=jnp.float32)  30.3 us
    dot_general x3, matrix products, column_proj(): jnp.einsum('bsr,bre->bse', value_a8, b_sel, preferred_element_type=jnp.fl...  27.6 us
  transfers between devices with their start and end apart: 4, of which 4 were waited for; matrix products, arithmetic and copies ran while one was open for 1% of the time, Pallas kernels for 0%

commit v1 on v0

v1 whole, which is shorter than its diff:
```python
import functools

import jax
import jax.numpy as jnp
from jax import lax
from jax.experimental import pallas as pl
from jax.experimental.pallas import tpu as pltpu
from jax.sharding import PartitionSpec as P

value_a10 = 16
RMS_EPS = 1e-5
F32 = jnp.float32
BF16 = jnp.bfloat16
MESH = pl.DeviceIdType.MESH
ANY = pl.BlockSpec(memory_space=pl.ANY)
VMEM = pl.BlockSpec(memory_space=pltpu.VMEM)
VMEM_LIMIT = 67043328
LANES = 128
CHIPS = 4
LAG = 6


def rms_scale(x_in, gain_vec):
    x_f32 = x_in.astype(F32)
    inv_rms = lax.rsqrt(jnp.mean(x_f32 * x_f32, axis=-1, keepdims=True) + RMS_EPS)
    return (x_f32 * inv_rms * gain_vec).astype(BF16)


def causal_attention(q_flat, k_flat, v_flat, kv_heads, head_dim):
    num_seqs, seq_len = q_flat.shape[0], q_flat.shape[1]
    q_group = q_flat.reshape(num_seqs, seq_len, kv_heads, -1, head_dim)
    k_group = k_flat.reshape(num_seqs, seq_len, kv_heads, head_dim)
    v_group = v_flat.reshape(num_seqs, seq_len, kv_heads, head_dim)
    scores = jnp.einsum('bqngd,bknd->bngqk', q_group, k_group, preferred_element_type=F32) * head_dim ** -0.5
    causal = jnp.arange(seq_len)[:, None] >= jnp.arange(seq_len)[None, :]
    prob_bf = jax.nn.softmax(jnp.where(causal, scores, -jnp.inf), axis=-1).astype(BF16)
    att_out = jnp.einsum('bngqk,bknd->bqngd', prob_bf, v_group, preferred_element_type=F32)
    return att_out.astype(BF16).reshape(num_seqs, seq_len, -1)


class Exchange:
    def __init__(self, part, recv0, recv1, recv2, quart, done, out, sems):
        self.part, self.recv0, self.recv1, self.recv2 = part, recv0, recv1, recv2
        self.quart, self.done, self.out = quart, done, out
        (self.s0, self.r0, self.s1, self.r1, self.s2, self.r2, self.sa, self.ra, self.sb, self.rb, self.sc, self.rc,
         self.own) = sems
        me = lax.axis_index('tp')
        self.chip, self.core = me // 2, me % 2
        self.half = part.shape[0] // 2
        self.rows = self.half // CHIPS
        self.hrows = self.rows // 2
        self.right = self.device(self.chip + 1, self.core)
        self.left = self.device(self.chip + CHIPS - 1, self.core)
        self.partner = self.device(self.chip, 1 - self.core)

    def device(self, chip, core):
        return (chip % CHIPS) * 2 + core

    @staticmethod
    def scratch(seq_len, width, done_width):
        half = seq_len // 2
        rows = half // CHIPS
        dma = pltpu.SemaphoreType.DMA
        return [pltpu.VMEM((seq_len, width), BF16), pltpu.VMEM((2, half, width), BF16),
                pltpu.VMEM((2, 2, rows // 2, width), BF16), pltpu.VMEM((2, 2, rows, width), BF16),
                pltpu.VMEM((3, half, width), BF16), pltpu.VMEM((2, rows, done_width), BF16),
                dma((2,)), dma((2,)), dma((2, 2)), dma((2, 2)), dma((2, 2)), dma((2, 2)),
                dma((3, 2)), dma((3, 2)), dma((4, 2)), dma((4, 2)), dma((2,)), dma((2,)), dma((2,))]

    def barrier(self):
        sem = pltpu.get_barrier_semaphore()
        for other in (self.right, self.left, self.partner):
            pl.semaphore_signal(sem, inc=1, device_id={'tp': other}, device_id_type=MESH)
        pl.semaphore_wait(sem, 3)

    def send(self, src, dst, send_sem, recv_sem, other):
        return pltpu.make_async_remote_copy(src_ref=src, dst_ref=dst, send_sem=send_sem, recv_sem=recv_sem,
                                            device_id={'tp': other}, device_id_type=MESH)

    def slab(self, step):
        return pl.multiple_of(((self.chip + step) % CHIPS) * self.rows, self.rows)

    def own_row(self):
        return pl.multiple_of(self.core * self.half + self.slab(0), self.rows)

    def copy0(self, c):
        first = pl.multiple_of((1 - self.core) * self.half, self.half)
        return [self.send(self.part.at[pl.ds(first, self.half)], self.recv0.at[c % 2], self.s0.at[c % 2],
                          self.r0.at[c % 2], self.partner)]

    def copy1(self, c):
        quart, far = self.quart.at[c % 3], self.slab(2)
        low = pl.multiple_of(far + self.hrows, self.hrows)
        return [self.send(quart.at[pl.ds(far, self.hrows)], self.recv1.at[0, c % 2], self.s1.at[0, c % 2],
                          self.r1.at[0, c % 2], self.right),
                self.send(quart.at[pl.ds(low, self.hrows)], self.recv1.at[1, c % 2], self.s1.at[1, c % 2],
                          self.r1.at[1, c % 2], self.left)]

    def copy2(self, c):
        quart = self.quart.at[c % 3]
        return [self.send(quart.at[pl.ds(self.slab(1), self.rows)], self.recv2.at[0, c % 2], self.s2.at[0, c % 2],
                          self.r2.at[0, c % 2], self.right),
                self.send(quart.at[pl.ds(self.slab(CHIPS - 1), self.rows)], self.recv2.at[1, c % 2],
                          self.s2.at[1, c % 2], self.r2.at[1, c % 2], self.left)]

    def copy_a(self, c):
        dst = self.out.at[c, pl.ds(self.own_row(), self.rows)]
        return [self.send(self.done.at[c % 2], dst, self.sa.at[i, c % 2], self.ra.at[i, c % 2], other)
                for i, other in enumerate((self.right, self.left, self.partner))]

    def copy_own(self, c):
        return pltpu.make_async_copy(self.done.at[c % 2], self.out.at[c, pl.ds(self.own_row(), self.rows)],
                                     self.own.at[c % 2])

    def copy_b(self, c):
        base = self.core * self.half
        from_left = pl.multiple_of(base + self.slab(CHIPS - 1), self.rows)
        from_right = pl.multiple_of(base + self.slab(1), self.rows)
        low = pl.multiple_of(from_right + self.hrows, self.hrows)
        parts = ((from_left, self.hrows, self.right), (low, self.hrows, self.left),
                 (from_left, self.rows, self.partner), (from_right, self.rows, self.partner))
        return [self.send(self.out.at[c, pl.ds(first, size)], self.out.at[c, pl.ds(first, size)],
                          self.sb.at[i, c % 2], self.rb.at[i, c % 2], other)
                for i, (first, size, other) in enumerate(parts)]

    def copy_c(self, c):
        far = pl.multiple_of(self.core * self.half + self.slab(2), self.rows)
        rows = self.out.at[c, pl.ds(far, self.rows)]
        return [self.send(rows, rows, self.sc.at[c % 2], self.rc.at[c % 2], self.partner)]

    @staticmethod
    def start(copies):
        for copy in copies:
            copy.start()

    @staticmethod
    def wait_send(copies):
        for copy in copies:
            copy.wait_send()

    @staticmethod
    def wait_recv(copies):
        for copy in copies:
            copy.wait_recv()

    def add_pair(self, c):
        self.wait_recv(self.copy0(c))
        self.wait_send(self.copy0(c))
        quart, recv = self.quart.at[c % 3], self.recv0.at[c % 2]
        own = self.core * self.half

        @pl.loop(0, self.half // 16)
        def _(i):
            mine = self.part[pl.ds(pl.multiple_of(own + i * 16, 16), 16), :].astype(F32)
            rows = pl.ds(pl.multiple_of(i * 16, 16), 16)
            quart[rows, :] = (mine + recv[rows, :].astype(F32)).astype(BF16)

        self.start(self.copy1(c))

    def add_far(self, c):
        self.wait_recv(self.copy1(c))
        quart = self.quart.at[c % 3]
        for side, first in ((0, self.slab(1)), (1, self.slab(CHIPS - 1) + self.hrows)):
            rows = pl.ds(pl.multiple_of(first, self.hrows), self.hrows)
            quart[rows, :] = (quart[rows, :].astype(F32) + self.recv1[side, c % 2].astype(F32)).astype(BF16)
        self.start(self.copy2(c))

    def finish(self, c, finalize):
        self.wait_recv(self.copy2(c))
        self.wait_send(self.copy1(c))
        quart, slot = self.quart.at[c % 3], c % 2

        def total(first, size, columns):
            rows = pl.ds(pl.multiple_of(self.slab(0) + first, size), size)
            here = pl.ds(first, size)
            return (quart[rows, columns].astype(F32) + self.recv2[0, slot, here, columns].astype(F32)
                    + self.recv2[1, slot, here, columns].astype(F32))

        finalize(c, total, self.done.at[slot])
        self.start(self.copy_a(c))
        self.copy_own(c).start()

    def forward(self, c):
        self.wait_recv(self.copy_a(c))
        self.wait_send(self.copy2(c))
        self.start(self.copy_b(c))

    def cross(self, c):
        self.wait_recv(self.copy_b(c))
        self.wait_send(self.copy_a(c))
        self.copy_own(c).wait()
        self.start(self.copy_c(c))

    def close(self, c):
        self.wait_recv(self.copy_c(c))
        self.wait_send(self.copy_b(c))
        self.wait_send(self.copy_c(c))

    def stages(self, slot, count, compute, finalize, prefetch=None):
        def far(c):
            if prefetch is not None:
                prefetch(c)
            self.add_far(c)

        table = ((6, self.close), (5, self.cross), (4, self.forward),
                 (3, lambda c: self.finish(c, finalize)), (2, far), (1, self.add_pair))
        for lag, stage in table:
            @pl.when((slot >= lag) & (slot < count + lag))
            def _(lag=lag, stage=stage):
                stage(slot - lag)

        @pl.when(slot < count)
        def _():
            compute(slot)
            self.start(self.copy0(slot))


def lora_rows(mid, mask_row, b_ref, c, columns, rank):
    lane = lax.broadcasted_iota(jnp.int32, mid.shape, 1)
    mid = mid.astype(BF16).astype(F32)
    out = None
    for r in range(rank):
        keep = (mask_row > 0) & (lane % rank == r)
        column = jnp.sum(jnp.where(keep, mid, 0.0), axis=1, keepdims=True)
        term = column * b_ref[c, r:r + 1, columns].astype(F32)
        out = term if out is None else out + term
    return out


def out_kernel(count, scale, rank, att_ref, wo_ref, ao_ref, bo_ref, mask_ref, res_ref, gain_ref, h2_ref, x1_ref,
               *scratch):
    exchange = Exchange(*scratch[:6], h2_ref, scratch[6:19])
    exchange.barrier()
    width = wo_ref.shape[1]
    tile = 512

    def compute(c):
        att = att_ref[c]

        @pl.loop(0, width // tile)
        def _(n):
            columns = pl.ds(pl.multiple_of(n * tile, tile), tile)
            exchange.part[:, columns] = jnp.dot(att, wo_ref[:, columns], preferred_element_type=F32).astype(BF16)

        exchange.part[:, width:] = lax.dot_general(att, ao_ref[...], (((1,), (1,)), ((), ())),
                                                   preferred_element_type=F32).astype(BF16)

    def finalize(c, total, done):
        mask_row = mask_ref[pl.ds(c, 1), :]
        for first in range(0, exchange.rows, 16):
            here = pl.ds(first, 16)
            mid = total(first, 16, pl.ds(width, LANES))
            square = jnp.zeros((16, 1), F32)
            for n in range(width // tile):
                columns = pl.ds(n * tile, tile)
                lora = lora_rows(mid, mask_row, bo_ref, c, columns, rank)
                x_one = (res_ref[c, here, columns].astype(F32) + (total(first, 16, columns) + scale * lora)).astype(BF16)
                x1_ref[c, here, columns] = x_one
                x_one = x_one.astype(F32)
                square += jnp.sum(x_one * x_one, axis=1, keepdims=True)
            inv_rms = lax.rsqrt(square / width + RMS_EPS)
            for n in range(width // tile):
                columns = pl.ds(n * tile, tile)
                x_one = x1_ref[c, here, columns].astype(F32)
                done[here, columns] = (x_one * inv_rms * gain_ref[:, columns]).astype(BF16)

    @pl.loop(0, count + LAG)
    def _(slot):
        exchange.stages(slot, count, compute, finalize)


def mlp_kernel(count, scale, rank, h2_ref, wg_ref, wu_ref, wd_ref, agu_ref, bg_ref, bu_ref, gmask_ref, ad_ref, bd_ref,
               mask_ref, res_ref, y_ref, *scratch):
    exchange = Exchange(*scratch[:6], y_ref, scratch[6:19])
    wg, wu, wd, hbuf, mid_buf, t_buf, rbuf, sem_g, sem_u, sem_d, sem_h, sem_r = scratch[19:]
    gtile, dtile = wg.shape[2], wd.shape[2]
    width = wd_ref.shape[1]

    def load_h(c):
        return pltpu.make_async_copy(h2_ref.at[c], hbuf, sem_h)

    def load_r(c):
        return pltpu.make_async_copy(res_ref.at[c], rbuf.at[c % 2], sem_r.at[c % 2])

    def load_g(j):
        columns = pl.ds(pl.multiple_of(j * gtile, gtile), gtile)
        return (pltpu.make_async_copy(wg_ref.at[:, columns], wg.at[j], sem_g.at[j]),
                pltpu.make_async_copy(wu_ref.at[:, columns], wu.at[j], sem_u.at[j]))

    def load_d(n):
        columns = pl.ds(pl.multiple_of(n * dtile, dtile), dtile)
        return pltpu.make_async_copy(wd_ref.at[:, columns], wd.at[n], sem_d.at[n])

    load_h(0).start()
    for j in range(wg.shape[0]):
        for copy in load_g(j):
            copy.start()
    for n in range(wd.shape[0]):
        load_d(n).start()
    exchange.barrier()

    def compute(c):
        load_h(c).wait()
        t_all = lax.dot_general(hbuf[...], agu_ref[...], (((1,), (1,)), ((), ())), preferred_element_type=F32)
        t_buf[...] = jnp.where(gmask_ref[pl.ds(c, 1), :] > 0, t_all.astype(BF16).astype(F32), 0.0).astype(BF16)

        @pl.loop(0, wg.shape[0])
        def _(j):
            @pl.when(c == 0)
            def _():
                for copy in load_g(j):
                    copy.wait()
            columns = pl.ds(pl.multiple_of(j * gtile, gtile), gtile)
            gate = jnp.dot(hbuf[...], wg[j], preferred_element_type=F32)
            gate += scale * jnp.dot(t_buf[...], bg_ref[:, columns], preferred_element_type=F32)
            gate = gate.astype(BF16).astype(F32)
            up = jnp.dot(hbuf[...], wu[j], preferred_element_type=F32)
            up += scale * jnp.dot(t_buf[...], bu_ref[:, columns], preferred_element_type=F32)
            up = up.astype(BF16).astype(F32)
            mid_buf[:, columns] = (jax.nn.silu(gate) * up).astype(BF16)

        @pl.when(c + 1 < count)
        def _():
            load_h(c + 1).start()

        @pl.loop(0, wd.shape[0])
        def _(n):
            @pl.when(c == 0)
            def _():
                load_d(n).wait()
            columns = pl.ds(pl.multiple_of(n * dtile, dtile), dtile)
            exchange.part[:, columns] = jnp.dot(mid_buf[...], wd[n], preferred_element_type=F32).astype(BF16)

        exchange.part[:, width:] = lax.dot_general(mid_buf[...], ad_ref[...], (((1,), (1,)), ((), ())),
                                                   preferred_element_type=F32).astype(BF16)

    def finalize(c, total, done):
        load_r(c).wait()
        mask_row = mask_ref[pl.ds(c, 1), :]
        for first in range(0, exchange.rows, 16):
            here = pl.ds(first, 16)
            mid = total(first, 16, pl.ds(width, LANES))
            for n in range(width // 512):
                columns = pl.ds(n * 512, 512)
                lora = lora_rows(mid, mask_row, bd_ref, c, columns, rank)
                res = rbuf[c % 2, here, columns].astype(F32)
                done[here, columns] = (res + (total(first, 16, columns) + scale * lora)).astype(BF16)

    @pl.loop(0, count + LAG)
    def _(slot):
        exchange.stages(slot, count, compute, finalize, lambda c: load_r(c).start())


def solution(mesh):
    act_spec = P('dp', None, None)
    w_head_spec = P(None, 'tp', None)
    w_out_spec = P('tp', None, None)
    w_col_spec = P(None, 'tp')
    w_row_spec = P('tp', None)
    a_rank_spec = P(None, None, 'tp')
    b_head_spec = P(None, None, 'tp', None)
    b_col_spec = P(None, None, 'tp')
    a_head_spec = P(None, 'tp', None, None)
    a_row_spec = P(None, 'tp', None)
    in_specs = (act_spec, P('dp'), P(None), P(None), w_head_spec, w_head_spec, w_head_spec, w_out_spec,
                w_col_spec, w_col_spec, w_row_spec, a_rank_spec, b_head_spec, a_rank_spec, b_head_spec,
                a_rank_spec, b_head_spec, a_head_spec, b_col_spec, a_rank_spec, b_col_spec,
                a_rank_spec, b_col_spec, a_row_spec, b_col_spec)

    def local_layer(x_in, adapter_ids, gain_attn, gain_mlp, w_q, w_k, w_v, w_o, w_gate, w_up, w_down,
                    a_q, b_q, a_k, b_k, a_v, b_v, a_o, b_o, a_gate, b_gate, a_up, b_up, a_down, b_down):
        count, seq_len, width = x_in.shape
        adapters, rank = b_q.shape[:2]
        mixed = adapters * rank
        scale = value_a10 / rank
        ff = w_gate.shape[1]

        a_loc = jnp.stack([a.transpose(2, 0, 1) for a in (a_q, a_k, a_v, a_gate, a_up)], 1)
        cols = b_o.shape[2]
        packed = jnp.concatenate([a_loc.reshape(-1, cols), b_o.reshape(-1, cols), b_down.reshape(-1, cols)], 0)
        packed = lax.all_gather(packed, 'tp', axis=0)
        n_a = a_loc.size // cols
        a_all = packed[:, :n_a].reshape(-1, 5, adapters, width).transpose(1, 0, 2, 3).reshape(5, mixed, width)
        b_rows = packed[:, n_a:].reshape(-1, 2, adapters, rank, cols).transpose(1, 2, 3, 0, 4)
        b_rows = jnp.take(b_rows.reshape(2, adapters, rank, width), adapter_ids, axis=1)

        rank_major = jnp.arange(mixed) % adapters == adapter_ids[:, None]
        id_major = jnp.arange(mixed) // rank == adapter_ids[:, None]
        mask_row = jnp.pad(id_major, ((0, 0), (0, LANES - mixed))).astype(F32)
        mask_two = jnp.tile(rank_major, (1, 2)).astype(F32)

        h_norm = rms_scale(x_in, gain_attn)
        w_all = jnp.concatenate([w.reshape(width, -1) for w in (w_q, w_k, w_v)], 1)
        base = jnp.einsum('bsd,de->bse', h_norm, w_all, preferred_element_type=F32)
        mids = jnp.einsum('bsd,rd->bsr', h_norm, a_all[:3].reshape(-1, width), preferred_element_type=F32).astype(BF16)
        mids = jnp.where(jnp.tile(rank_major, (1, 3))[:, None], mids, jnp.zeros((), BF16))
        n_q, n_k = w_q[0].size, w_k[0].size
        b_all = [b.transpose(1, 0, 2, 3).reshape(mixed, -1) for b in (b_q, b_k, b_v)]
        b_all = jnp.concatenate([jnp.pad(b, ((0, 0), (first, w_all.shape[1] - first - b.shape[1])))
                                 for b, first in zip(b_all, (0, n_q, n_q + n_k))], 0)
        qkv = (base + scale * jnp.einsum('bsr,re->bse', mids, b_all, preferred_element_type=F32)).astype(BF16)
        att = causal_attention(qkv[..., :n_q], qkv[..., n_q:n_q + n_k], qkv[..., n_q + n_k:], w_k.shape[1],
                               w_k.shape[2])

        me = lax.axis_index('tp')
        own = seq_len // 2 // CHIPS
        own_row = (me % 2) * (seq_len // 2) + (me // 2) * own
        res = lax.dynamic_slice_in_dim(x_in, own_row, own, axis=1)
        a_o_t = jnp.pad(a_o.transpose(0, 3, 1, 2).reshape(mixed, -1), ((0, LANES - mixed), (0, 0)))
        exchange_scratch = Exchange.scratch(seq_len, width + LANES, width)
        h_two, x_one = pl.pallas_call(
            functools.partial(out_kernel, count, scale, rank),
            out_shape=(jax.ShapeDtypeStruct(x_in.shape, BF16), jax.ShapeDtypeStruct(res.shape, BF16)),
            in_specs=[VMEM] * 7, out_specs=(ANY, VMEM), scratch_shapes=exchange_scratch,
            compiler_params=pltpu.CompilerParams(collective_id=0, has_side_effects=True, vmem_limit_bytes=VMEM_LIMIT),
        )(att, w_o.reshape(-1, width), a_o_t, b_rows[0], mask_row, res, gain_mlp.reshape(1, -1))

        b_cols = [b.transpose(1, 0, 2).reshape(mixed, -1) for b in (b_gate, b_up)]
        b_g = jnp.pad(b_cols[0], ((0, mixed), (0, 0)))
        b_u = jnp.pad(b_cols[1], ((mixed, 0), (0, 0)))
        a_d_t = jnp.pad(a_down.transpose(0, 2, 1).reshape(mixed, -1), ((0, LANES - mixed), (0, 0)))
        gtile, dtile = 256, 512
        dma = pltpu.SemaphoreType.DMA
        return pl.pallas_call(
            functools.partial(mlp_kernel, count, scale, rank),
            out_shape=jax.ShapeDtypeStruct(x_in.shape, BF16),
            in_specs=[ANY] * 4 + [VMEM] * 7 + [ANY], out_specs=ANY,
            scratch_shapes=exchange_scratch + [
                pltpu.VMEM((ff // gtile, width, gtile), BF16), pltpu.VMEM((ff // gtile, width, gtile), BF16),
                pltpu.VMEM((width // dtile, ff, dtile), BF16), pltpu.VMEM((seq_len, width), BF16),
                pltpu.VMEM((seq_len, ff), BF16), pltpu.VMEM((seq_len, 2 * mixed), BF16),
                pltpu.VMEM((2, own, width), BF16), dma((ff // gtile,)), dma((ff // gtile,)), dma((width // dtile,)),
                dma, dma((2,))],
            compiler_params=pltpu.CompilerParams(collective_id=1, has_side_effects=True, vmem_limit_bytes=VMEM_LIMIT),
        )(h_two, w_gate, w_up, w_down, a_all[3:].reshape(2 * mixed, width), b_g, b_u, mask_two, a_d_t, b_rows[1],
          mask_row, x_one)

    return jax.shard_map(local_layer, mesh=mesh, in_specs=in_specs, out_specs=act_spec, check_vma=False)
```

time: 745 us -> 492 us (0.66)
  Pallas kernels: 0 us -> 368 us
  waiting for transfers between devices: 289 us -> 0.06 us
  matrix products: 261 us -> 37.1 us
  blocking collectives: 112 us -> 0 us
  local copies, waits for them, and re-layouts: 40.8 us -> 57.9 us
  other arithmetic: 22.8 us -> 13.4 us
    pallas_call x0 -> x2, Pallas kernels: none -> 368 us  [the longest x1 208 us: local_layer(): pl.pallas_call(functools.partial(mlp_kernel, count, scale, rank), out_sha...]
    dot_general x19 -> x2, matrix products: 250 us -> 30.5 us  [the longest x1 18.6 us: local_layer(): base = jnp.einsum('bsd,de->bse', h_norm, w_all, preferred_element_type=F32)]
    all_gather x2 -> x1, waiting for transfers between devices: 164 us -> 0.01 us  [local_layer(): packed = lax.all_gather(packed, 'tp', axis=0)]
    reduce_scatter x2 -> x0, waiting for transfers between devices: 125 us -> none  [row_proj(): lax.psum_scatter(base_part, 'tp', scatter_dimension=2, tiled=True)]
    all_gather x5 -> x0, blocking collectives: 67.6 us -> none  [column_proj(): value_a8 = lax.all_gather(value_a9, 'tp', axis=2, tiled=True)]
    psum x2 -> x0, blocking collectives: 44.2 us -> none  [row_proj(): value_a8 = lax.psum(value_a9, 'tp')]
    slice x0 -> x7, local copies, waits for them, and re-layouts: none -> 12.3 us  [the longest x2 4.21 us: local_layer(): packed[:, n_a:].reshape(-1, 2, adapters, rank, cols)]
    gather x15 -> x1, local copies, waits for them, and re-layouts: 12.9 us -> 1.84 us  [local_layer(): jnp.take(b_rows.reshape(2, adapters, rank, width), adapter_ids, axis=1)]
  transfers between devices with their start and end apart: 4 -> 1, of which waited for: 4 -> 0; matrix products, arithmetic and copies ran while one was open for 1% -> 9% of each run, Pallas kernels for 0% -> 0%
where the time goes in v1:
time: 492 us; the launch traced here: 491 us
  Pallas kernels  368 us (75%)
  local copies, waits for them, and re-layouts  57.9 us (12%)
  matrix products  37.1 us (8%)
  between operations  13.7 us (3%)
  other arithmetic  13.4 us (3%)
    pallas_call x1, Pallas kernels, local_layer(): pl.pallas_call(functools.partial(mlp_kernel, count, scale, rank), out_sha...  208 us
    pallas_call x1, Pallas kernels, local_layer(): pl.pallas_call(functools.partial(out_kernel, count, scale, rank), out_sha...  160 us
    unnamed x22, local copies, waits for them, and re-layouts  22.4 us
    dot_general x1, matrix products, local_layer(): base = jnp.einsum('bsd,de->bse', h_norm, w_all, preferred_element_type=F32)  18.6 us
    dot_general x1, matrix products, local_layer(): jnp.einsum('bsr,re->bse', mids, b_all, preferred_element_type=F32)  11.8 us
  transfers between devices with their start and end apart: 1, of which 0 were waited for; matrix products, arithmetic and copies ran while one was open for 9% of the time, Pallas kernels for 0%

profile of v1, /device:TPU:81, one launch (start us, length us, event | category | flops | bytes accessed | tf_op | source)
XLA Modules:
  0.0 490.5 jit_solution(9863452044378080314)
XLA Ops:
  10.9 1.7 pad_maximum_fusion
  16.1 1.5 pad.34.ao_ref
  20.2 1.8 pad.38.ad_ref
  22.0 4.9 %copy.83 = bf16[512,8,4,128]{3,1,2,0:T(8,128)(2,1)} copy(bf16[512,8,4,128]{3,2,1,0:T(4,128)(2,1)} %bitcast.119) | data formatting | bytes 8388608
  27.6 8.3 %fusion = f32[8,256]{1,0:T(8,128)S(1)} fusion(bf16[8,256,4096]{2,1,0:T(8,128)(2,1)} %param.25), kind=kLoop, calls=%fused_computation.3 | loop fusion | flops 25163776 | bytes 16785408 | tf_op jit(solution)/shard_map/reduce_sum | solution.py:25
  36.0 3.2 constant_dynamic-slice_fusion.res_ref
  39.1 18.6 %fusion.5 = f32[8,256,768]{2,1,0:T(8,128)} fusion(bf16[8,256,4096]{2,1,0:T(8,128)(2,1)} %param.25, f32[4096]{0:T(1024)S(1)} %copy-done.7, f32[8,256]{1,0:T(8,128)S(1)} %add_rsqrt_fusion, bf16[4096,128]{1,0:T(8,128)(2,1)S(1)} %bitcast.140, bf16[4096,128]{1,0:T(8,128)(2,1)S(1)} %bitcast.141, bf16[4096,512]{1,0:T(8,128)(2,1)S(1)} %bitcast.121), kind=kOutput, calls=%fused_computation.7 | convolution fusion | flops 12937330688 | bytes 29384704 | tf_op jit(solution)/shard_map/bsd,de->bse/dot_general | solution.py:394
  57.8 2.3 slice.45
  60.1 3.4 slice.40
  63.5 3.9 reshape.174
  67.4 1.0 slice.47
  68.4 1.3 slice.41
  69.7 1.9 copy.55
  71.6 1.3 reshape.185
  72.9 1.8 gather_fusion
  76.1 2.3 copy.57
  78.4 11.8 %add_convert_fusion = bf16[8,256,768]{2,1,0:T(8,128)(2,1)} fusion(f32[8,256,768]{2,1,0:T(8,128)} %fusion.5, bf16[192,4096,1]{1,0,2:T(8,128)(2,1)S(1)} %bitcast.126, bf16[8,256,4096]{2,1,0:T(8,128)(2,1)} %param.25, f32[4096]{0:T(1024)S(1)} %copy-done.7, f32[8,256]{1,0:T(8,128)S(1)} %add_rsqrt_fusion, pred[8,192]{1,0:T(8,128)(4,1)S(1)} %tile.7, ...), kind=kOutput, calls=%fused_computation.18 | convolution fusion | flops 3866329088 | bytes 27911680 | tf_op jit(solution)/shard_map/bsr,re->bse/dot_general | solution.py:401
  90.2 3.1 fusion.8
  93.3 1.9 fusion.7
  95.2 3.6 fusion.19
  98.8 2.4 copy.65.att_ref
  101.2 159.9 %shard_map.235 = (bf16[8,256,4096]{2,1,0:T(8,128)(2,1)}, bf16[8,32,4096]{2,1,0:T(8,128)(2,1)}) custom-call(bf16[8,256,512]{2,1,0:T(8,128)(2,1)} %copy.65.att_ref, bf16[512,4096]{1,0:T(8,128)(2,1)} %bitcast.120, bf16[128,512]{1,0:T(8,128)(2,1)} %pad.34.ao_ref, bf16[8,8,4096]{2,1,0:T(8,128)(2,1)} %get-tuple-element.10.bo_ref, ...), custom_call_target="tpu_custom_call" | custom-call | tf_op jit(solution)/shard_map/pallas_call | solution.py:411
  261.1 208.5 %shard_map.236 = bf16[8,256,4096]{2,1,0:T(8,128)(2,1)} custom-call(bf16[8,256,4096]{2,1,0:T(8,128)(2,1)} %get-tuple-element.7.h2_ref, bf16[4096,1792]{1,0:T(8,128)(2,1)} %wg_ref.1, bf16[4096,1792]{1,0:T(8,128)(2,1)} %wu_ref.1, bf16[1792,4096]{1,0:T(8,128)(2,1)} %wd_ref.1, bf16[128,4096]{1,0:T(8,128)(2,1)} %bitcast.118, bf16[128,1792]{1,0:T(8,128)(2,1)} %pad.36.bg_ref, ...), custom_call_target="tpu_custom_call" | custom-call | tf_op jit(solution)/shard_map/pallas_call | solution.py:424
  469.6 14.1 %copy.92 = bf16[8,256,4096]{2,1,0:T(8,128)(2,1)} copy(bf16[8,256,4096]{2,1,0:T(8,128)(2,1)} %shard_map.236) | data formatting | bytes 33554432
  (46 shorter events, 12.4 us)
Async XLA Ops:
  6.5 20.3 %copy-start.4 = (s32[8]{0:T(128)S(1)}, s32[8]{0:T(128)}, u32[]{:S(2)}) copy-start(s32[8]{0:T(128)} %param.26) | copy-start | bytes 100
  6.5 51.2 %all-gather.3.cloned.1.call-start = ((), (), s32[]{:S(2)}) async-start(), calls=%async_computation | async-start | bytes 4128768 | tf_op jit(solution)/shard_map/all_gather | solution.py:381
  27.5 8.4 %copy-start.2 = (bf16[8,8,1,128]{3,1,2,0:T(8,128)(2,1)S(1)}, bf16[8,8,1,128]{3,1,2,0:T(8,128)(2,1)}, u32[]{:S(2)}) copy-start(bf16[8,8,1,128]{3,1,2,0:T(8,128)(2,1)} %param.41) | copy-start | bytes 49156
  27.5 8.4 %copy-start.3 = (bf16[8,8,1,128]{3,1,2,0:T(8,128)(2,1)S(1)}, bf16[8,8,1,128]{3,1,2,0:T(8,128)(2,1)}, u32[]{:S(2)}) copy-start(bf16[8,8,1,128]{3,1,2,0:T(8,128)(2,1)} %param.39) | copy-start | bytes 49156
  27.5 11.6 %copy-start.1 = (bf16[512,8,4,128]{3,1,2,0:T(8,128)(2,1)S(1)}, bf16[512,8,4,128]{3,1,2,0:T(8,128)(2,1)}, u32[]{:S(2)}) copy-start(bf16[512,8,4,128]{3,1,2,0:T(8,128)(2,1)} %copy.83) | copy-start | bytes 12582916
  27.6 11.6 %copy-start.5 = (bf16[4096,1,128]{2,0,1:T(8,128)(2,1)S(1)}, bf16[4096,1,128]{2,0,1:T(8,128)(2,1)}, u32[]{:S(2)}) copy-start(bf16[4096,1,128]{2,0,1:T(8,128)(2,1)} %param.31) | copy-start | bytes 3145732
  27.6 11.6 %copy-start.6 = (bf16[4096,1,128]{2,0,1:T(8,128)(2,1)S(1)}, bf16[4096,1,128]{2,0,1:T(8,128)(2,1)}, u32[]{:S(2)}) copy-start(bf16[4096,1,128]{2,0,1:T(8,128)(2,1)} %param.30) | copy-start | bytes 3145732
  27.6 11.6 %copy-start.7 = (f32[4096]{0:T(1024)S(1)}, f32[4096]{0:T(1024)}, u32[]{:S(2)}) copy-start(f32[4096]{0:T(1024)} %param.27) | copy-start | bytes 49156
  69.7 6.3 %copy-start = (bf16[3,8,8,4096]{3,2,0,1:T(8,128)(2,1)S(1)}, bf16[3,8,8,4096]{3,2,0,1:T(8,128)(2,1)}, u32[]{:S(2)}) copy-start(bf16[3,8,8,4096]{3,2,0,1:T(8,128)(2,1)} %slice.41) | copy-start | bytes 4718596
Sparse Core Ops, SparseCore 0:
  12.8 31.1 all-gather.2

commit v2 on v1

v2 whole, which is shorter than its diff:
```python
import functools

import jax
import jax.numpy as jnp
from jax import lax
from jax.experimental import pallas as pl
from jax.experimental.pallas import tpu as pltpu
from jax.sharding import PartitionSpec as P

value_a10 = 16
RMS_EPS = 1e-5
F32 = jnp.float32
BF16 = jnp.bfloat16
MESH = pl.DeviceIdType.MESH
ANY = pl.BlockSpec(memory_space=pl.ANY)
VMEM = pl.BlockSpec(memory_space=pltpu.VMEM)
VMEM_LIMIT = 67043328
LANES = 128
CHIPS = 4
LAG = 6


class Exchange:
    def __init__(self, part, recv0, recv1, recv2, quart, done, out, sems):
        self.part, self.recv0, self.recv1, self.recv2 = part, recv0, recv1, recv2
        self.quart, self.done, self.out = quart, done, out
        (self.s0, self.r0, self.s1, self.r1, self.s2, self.r2, self.sa, self.ra, self.sb, self.rb, self.sc, self.rc,
         self.own) = sems
        me = lax.axis_index('tp')
        self.chip, self.core = me // 2, me % 2
        self.half = part.shape[0] // 2
        self.rows = self.half // CHIPS
        self.hrows = self.rows // 2
        self.right = self.device(self.chip + 1, self.core)
        self.left = self.device(self.chip + CHIPS - 1, self.core)
        self.partner = self.device(self.chip, 1 - self.core)

    def device(self, chip, core):
        return (chip % CHIPS) * 2 + core

    @staticmethod
    def scratch(seq_len, width, done_width):
        half = seq_len // 2
        rows = half // CHIPS
        dma = pltpu.SemaphoreType.DMA
        return [pltpu.VMEM((seq_len, width), BF16), pltpu.VMEM((2, half, width), BF16),
                pltpu.VMEM((2, 2, rows // 2, width), BF16), pltpu.VMEM((2, 2, rows, width), BF16),
                pltpu.VMEM((3, half, width), BF16), pltpu.VMEM((2, rows, done_width), BF16),
                dma((2,)), dma((2,)), dma((2, 2)), dma((2, 2)), dma((2, 2)), dma((2, 2)),
                dma((3, 2)), dma((3, 2)), dma((4, 2)), dma((4, 2)), dma((2,)), dma((2,)), dma((2,))]

    def barrier(self):
        sem = pltpu.get_barrier_semaphore()
        for other in (self.right, self.left, self.partner):
            pl.semaphore_signal(sem, inc=1, device_id={'tp': other}, device_id_type=MESH)
        pl.semaphore_wait(sem, 3)

    def send(self, src, dst, send_sem, recv_sem, other):
        return pltpu.make_async_remote_copy(src_ref=src, dst_ref=dst, send_sem=send_sem, recv_sem=recv_sem,
                                            device_id={'tp': other}, device_id_type=MESH)

    def slab(self, step):
        return pl.multiple_of(((self.chip + step) % CHIPS) * self.rows, self.rows)

    def own_row(self):
        return pl.multiple_of(self.core * self.half + self.slab(0), self.rows)

    def copy0(self, c):
        first = pl.multiple_of((1 - self.core) * self.half, self.half)
        return [self.send(self.part.at[pl.ds(first, self.half)], self.recv0.at[c % 2], self.s0.at[c % 2],
                          self.r0.at[c % 2], self.partner)]

    def copy1(self, c):
        quart, far = self.quart.at[c % 3], self.slab(2)
        low = pl.multiple_of(far + self.hrows, self.hrows)
        return [self.send(quart.at[pl.ds(far, self.hrows)], self.recv1.at[0, c % 2], self.s1.at[0, c % 2],
                          self.r1.at[0, c % 2], self.right),
                self.send(quart.at[pl.ds(low, self.hrows)], self.recv1.at[1, c % 2], self.s1.at[1, c % 2],
                          self.r1.at[1, c % 2], self.left)]

    def copy2(self, c):
        quart = self.quart.at[c % 3]
        return [self.send(quart.at[pl.ds(self.slab(1), self.rows)], self.recv2.at[0, c % 2], self.s2.at[0, c % 2],
                          self.r2.at[0, c % 2], self.right),
                self.send(quart.at[pl.ds(self.slab(CHIPS - 1), self.rows)], self.recv2.at[1, c % 2],
                          self.s2.at[1, c % 2], self.r2.at[1, c % 2], self.left)]

    def copy_a(self, c):
        dst = self.out.at[c, pl.ds(self.own_row(), self.rows)]
        return [self.send(self.done.at[c % 2], dst, self.sa.at[i, c % 2], self.ra.at[i, c % 2], other)
                for i, other in enumerate((self.right, self.left, self.partner))]

    def copy_own(self, c):
        return pltpu.make_async_copy(self.done.at[c % 2], self.out.at[c, pl.ds(self.own_row(), self.rows)],
                                     self.own.at[c % 2])

    def copy_b(self, c):
        base = self.core * self.half
        from_left = pl.multiple_of(base + self.slab(CHIPS - 1), self.rows)
        from_right = pl.multiple_of(base + self.slab(1), self.rows)
        low = pl.multiple_of(from_right + self.hrows, self.hrows)
        parts = ((from_left, self.hrows, self.right), (low, self.hrows, self.left),
                 (from_left, self.rows, self.partner), (from_right, self.rows, self.partner))
        return [self.send(self.out.at[c, pl.ds(first, size)], self.out.at[c, pl.ds(first, size)],
                          self.sb.at[i, c % 2], self.rb.at[i, c % 2], other)
                for i, (first, size, other) in enumerate(parts)]

    def copy_c(self, c):
        far = pl.multiple_of(self.core * self.half + self.slab(2), self.rows)
        rows = self.out.at[c, pl.ds(far, self.rows)]
        return [self.send(rows, rows, self.sc.at[c % 2], self.rc.at[c % 2], self.partner)]

    @staticmethod
    def start(copies):
        for copy in copies:
            copy.start()

    @staticmethod
    def wait_send(copies):
        for copy in copies:
            copy.wait_send()

    @staticmethod
    def wait_recv(copies):
        for copy in copies:
            copy.wait_recv()

    def add_pair(self, c):
        self.wait_recv(self.copy0(c))
        self.wait_send(self.copy0(c))
        quart, recv = self.quart.at[c % 3], self.recv0.at[c % 2]
        own = self.core * self.half

        @pl.loop(0, self.half // 16)
        def _(i):
            mine = self.part[pl.ds(pl.multiple_of(own + i * 16, 16), 16), :].astype(F32)
            rows = pl.ds(pl.multiple_of(i * 16, 16), 16)
            quart[rows, :] = (mine + recv[rows, :].astype(F32)).astype(BF16)

        self.start(self.copy1(c))

    def add_far(self, c):
        self.wait_recv(self.copy1(c))
        quart = self.quart.at[c % 3]
        for side, first in ((0, self.slab(1)), (1, self.slab(CHIPS - 1) + self.hrows)):
            rows = pl.ds(pl.multiple_of(first, self.hrows), self.hrows)
            quart[rows, :] = (quart[rows, :].astype(F32) + self.recv1[side, c % 2].astype(F32)).astype(BF16)
        self.start(self.copy2(c))

    def finish(self, c, finalize):
        self.wait_recv(self.copy2(c))
        self.wait_send(self.copy1(c))
        quart, slot = self.quart.at[c % 3], c % 2

        def total(first, size, columns):
            rows = pl.ds(pl.multiple_of(self.slab(0) + first, size), size)
            here = pl.ds(first, size)
            return (quart[rows, columns].astype(F32) + self.recv2[0, slot, here, columns].astype(F32)
                    + self.recv2[1, slot, here, columns].astype(F32))

        finalize(c, total, self.done.at[slot])
        self.start(self.copy_a(c))
        self.copy_own(c).start()

    def forward(self, c):
        self.wait_recv(self.copy_a(c))
        self.wait_send(self.copy2(c))
        self.start(self.copy_b(c))

    def cross(self, c):
        self.wait_recv(self.copy_b(c))
        self.wait_send(self.copy_a(c))
        self.copy_own(c).wait()
        self.start(self.copy_c(c))

    def close(self, c):
        self.wait_recv(self.copy_c(c))
        self.wait_send(self.copy_b(c))
        self.wait_send(self.copy_c(c))

    def stages(self, slot, count, finalize, prefetch):
        def far(c):
            prefetch(c)
            self.add_far(c)

        table = ((6, self.close), (5, self.cross), (4, self.forward),
                 (3, lambda c: self.finish(c, finalize)), (2, far), (1, self.add_pair))
        for lag, stage in table:
            @pl.when((slot >= lag) & (slot < count + lag))
            def _(lag=lag, stage=stage):
                stage(slot - lag)


class Gather:
    def __init__(self, exchange, own, full, sems):
        self.ex, self.own, self.full = exchange, own, full
        self.sa, self.ra, self.sb, self.rb, self.sc, self.rc = sems
        self.rows = own.shape[1]
        self.half = self.rows // 2

    @staticmethod
    def scratch():
        dma = pltpu.SemaphoreType.DMA
        return [dma((2, 3)), dma((2, 3)), dma((2, 4)), dma((2, 4)), dma((2,)), dma((2,))]

    def first(self, device):
        return pl.multiple_of(device * self.rows, self.rows)

    def copy_a(self, p):
        ex = self.ex
        dst = self.full.at[p, pl.ds(self.first(ex.device(ex.chip, ex.core)), self.rows)]
        return [ex.send(self.own.at[p], dst, self.sa.at[p, i], self.ra.at[p, i], other)
                for i, other in enumerate((ex.right, ex.left, ex.partner))]

    def copy_b(self, p):
        ex = self.ex
        from_left, from_right = self.first(ex.left), self.first(ex.right)
        low = pl.multiple_of(from_right + self.half, self.half)
        parts = ((from_left, self.half, ex.right), (low, self.half, ex.left),
                 (from_left, self.rows, ex.partner), (from_right, self.rows, ex.partner))
        return [ex.send(self.full.at[p, pl.ds(first, size)], self.full.at[p, pl.ds(first, size)], self.sb.at[p, i],
                        self.rb.at[p, i], other) for i, (first, size, other) in enumerate(parts)]

    def copy_c(self, p):
        ex = self.ex
        rows = self.full.at[p, pl.ds(self.first(ex.device(ex.chip + 2, ex.core)), self.rows)]
        return [ex.send(rows, rows, self.sc.at[p], self.rc.at[p], ex.partner)]

    def begin(self, p):
        me = self.ex.device(self.ex.chip, self.ex.core)
        self.ex.start(self.copy_a(p))
        self.full[p, pl.ds(self.first(me), self.rows), :] = self.own[p]

    def forward(self, p):
        self.ex.wait_recv(self.copy_a(p))
        self.ex.start(self.copy_b(p))

    def cross(self, p):
        self.ex.wait_recv(self.copy_b(p))
        self.ex.start(self.copy_c(p))

    def close(self, p):
        self.ex.wait_recv(self.copy_c(p))
        for copies in (self.copy_a, self.copy_b, self.copy_c):
            self.ex.wait_send(copies(p))


def dot_t(a, b):
    return lax.dot_general(a, b, (((1,), (1,)), ((), ())), preferred_element_type=F32)


def dot(a, b):
    return jnp.dot(a, b, preferred_element_type=F32)


def layer_kernel(count, scale, rank, heads, head_dim, x_ref, wqkv_ref, wo_ref, wg_ref, wu_ref, wd_ref, own_ref,
                 bqkv_ref, bg_ref, bu_ref, ao_ref, ad_ref, masks_ref, amask_ref, gain_a_ref, gain_m_ref, y_ref, h2_ref,
                 *scratch):
    one = Exchange(*scratch[:6], h2_ref, scratch[6:19])
    two = Exchange(*scratch[19:25], y_ref, scratch[25:38])
    full = scratch[38]
    gather = Gather(one, own_ref, full, scratch[39:45])
    (wqkv, wo, wd, ring, ubuf, qkv, att, mid, t_buf, x1, rbuf, sem_w, sem_d, sem_ring, sem_x, sem_h, sem_r) = scratch[45:]
    seq_len, width = ubuf.shape
    gtile, dtile = ring.shape[2], wd.shape[2]
    pairs, downs = mid.shape[1] // gtile, wd.shape[0]
    mixed = full.shape[1]

    def load_x(c):
        return pltpu.make_async_copy(x_ref.at[c], ubuf, sem_x)

    def load_h(c):
        return pltpu.make_async_copy(h2_ref.at[c], ubuf, sem_h)

    def load_r(c):
        return pltpu.make_async_copy(x_ref.at[c, pl.ds(one.own_row(), one.rows)], rbuf.at[c % 2], sem_r.at[c % 2])

    def load_d(n):
        columns = pl.ds(pl.multiple_of(n * dtile, dtile), dtile)
        return pltpu.make_async_copy(wd_ref.at[:, columns], wd.at[n], sem_d.at[n])

    def load_tile(w_ref, c, j, side):
        place = ((c * pairs + j) * 2 + side) % 3
        columns = pl.ds(pl.multiple_of(j * gtile, gtile), gtile)
        return pltpu.make_async_copy(w_ref.at[:, columns], ring.at[place], sem_ring.at[place]), place

    load_qkv = pltpu.make_async_copy(wqkv_ref, wqkv, sem_w.at[0])
    load_o = pltpu.make_async_copy(wo_ref, wo, sem_w.at[1])

    load_x(0).start()
    load_qkv.start()
    load_o.start()
    one.barrier()
    gather.begin(0)
    gather.begin(1)
    for w_ref, j, side in ((wg_ref, 0, 0), (wu_ref, 0, 1), (wg_ref, 1, 0)):
        load_tile(w_ref, 0, j, side)[0].start()
    for n in range(downs):
        load_d(n).start()

    def attention(c):
        load_x(c).wait()

        @pl.loop(0, seq_len // 16)
        def _(i):
            rows = pl.ds(pl.multiple_of(i * 16, 16), 16)
            value = ubuf[rows, :].astype(F32)
            inv_rms = lax.rsqrt(jnp.sum(value * value, axis=1, keepdims=True) / width + RMS_EPS)
            ubuf[rows, :] = (value * inv_rms * gain_a_ref[...]).astype(BF16)

        @pl.when(c == 0)
        def _():
            gather.forward(0)
            gather.cross(0)
            load_qkv.wait()
            load_o.wait()
            gather.close(0)

        @pl.when(c == 1)
        def _():
            gather.forward(1)

        @pl.when(c == 2)
        def _():
            gather.cross(1)

        keep = masks_ref[c, :, 0:mixed] > 0
        t_buf[...] = jnp.where(keep, dot_t(ubuf[...], full[0]).astype(BF16).astype(F32), 0.0).astype(BF16)

        @pl.loop(0, qkv.shape[1] // 256)
        def _(n):
            columns = pl.ds(pl.multiple_of(n * 256, 256), 256)
            base = dot(ubuf[...], wqkv[:, columns])
            qkv[:, columns] = (base + scale * dot(t_buf[...], bqkv_ref[:, columns])).astype(BF16)

        @pl.when((c + 1 < count) & (c < LAG))
        def _():
            load_x(c + 1).start()

        kv_heads = (qkv.shape[1] // head_dim - heads) // 2
        causal = (lax.broadcasted_iota(jnp.int32, (seq_len, seq_len), 0)
                  >= lax.broadcasted_iota(jnp.int32, (seq_len, seq_len), 1))
        for j in range(heads):
            kv = heads + j * kv_heads // heads
            query, key, value = (qkv[:, i * head_dim:(i + 1) * head_dim] for i in (j, kv, kv + kv_heads))
            scores = jnp.where(causal, dot_t(query, key) * head_dim ** -0.5, -jnp.inf)
            prob = jnp.exp(scores - jnp.max(scores, axis=1, keepdims=True))
            prob = (prob / jnp.sum(prob, axis=1, keepdims=True)).astype(BF16)
            att[:, j * head_dim:(j + 1) * head_dim] = dot(prob, value).astype(BF16)

        @pl.loop(0, width // 512)
        def _(n):
            columns = pl.ds(pl.multiple_of(n * 512, 512), 512)
            one.part[:, columns] = dot(att[...], wo[:, columns]).astype(BF16)

        pad = jnp.zeros((seq_len, LANES - ao_ref.shape[0]), F32)
        one.part[:, width:] = jnp.concatenate([dot_t(att[...], ao_ref[...]), pad], 1).astype(BF16)

        @pl.when(c == 2)
        def _():
            gather.close(1)

    def mlp(c):
        load_h(c).wait()
        keep = masks_ref[c, :, mixed:2 * mixed] > 0
        t_buf[...] = jnp.where(keep, dot_t(ubuf[...], full[1]).astype(BF16).astype(F32), 0.0).astype(BF16)

        def product(w_ref, b_ref, j, side):
            copy, place = load_tile(w_ref, c, j, side)
            copy.wait()
            columns = pl.ds(pl.multiple_of(j * gtile, gtile), gtile)
            out = dot(ubuf[...], ring[place]) + scale * dot(t_buf[...], b_ref[:, columns])
            return out.astype(BF16)

        def refill(w_ref, j, side):
            wrap = j // pairs
            @pl.when(c + wrap < count)
            def _():
                load_tile(w_ref, c + wrap, j % pairs, side)[0].start()

        @pl.loop(0, pairs)
        def _(j):
            columns = pl.ds(pl.multiple_of(j * gtile, gtile), gtile)
            mid[:, columns] = product(wg_ref, bg_ref, j, 0)
            refill(wu_ref, j + 1, 1)
            up = product(wu_ref, bu_ref, j, 1)
            refill(wg_ref, j + 2, 0)
            mid[:, columns] = (jax.nn.silu(mid[:, columns].astype(F32)) * up.astype(F32)).astype(BF16)

        @pl.when(c + LAG + 1 < count)
        def _():
            load_x(c + LAG + 1).start()

        @pl.loop(0, downs)
        def _(n):
            @pl.when(c == 0)
            def _():
                load_d(n).wait()
            columns = pl.ds(pl.multiple_of(n * dtile, dtile), dtile)
            two.part[:, columns] = dot(mid[...], wd[n]).astype(BF16)

        pad = jnp.zeros((seq_len, LANES - ad_ref.shape[0]), F32)
        two.part[:, width:] = jnp.concatenate([dot_t(mid[...], ad_ref[...]), pad], 1).astype(BF16)

    def totals(c, total, exchange, first_b):
        tile = width // (mixed // own_ref.shape[1])
        lanes = total(0, exchange.rows, pl.ds(width, LANES)).astype(BF16).astype(F32)
        lane = lax.broadcasted_iota(jnp.int32, lanes.shape, 1)
        keep = masks_ref[c, :, 2 * mixed:2 * mixed + LANES] > 0
        lanes = jnp.where(keep, lanes, 0.0)
        columns = [jnp.sum(jnp.where(lane % rank == r, lanes, 0.0), axis=1, keepdims=True) for r in range(rank)]
        chosen = amask_ref[c] > 0
        for n in range(width // tile):
            lora = None
            for r in range(rank):
                b_all = full[1, n * own_ref.shape[1] + first_b:n * own_ref.shape[1] + first_b + 8,
                             r * tile:(r + 1) * tile].astype(F32)
                b_row = jnp.sum(jnp.where(chosen[:, :1], b_all, 0.0), axis=0, keepdims=True)
                lora = columns[r] * b_row if lora is None else lora + columns[r] * b_row
            yield pl.ds(n * tile, tile), total(0, exchange.rows, pl.ds(n * tile, tile)) + scale * lora

    def finish_one(c, total, done):
        load_r(c).wait()
        square = jnp.zeros((one.rows, 1), F32)
        for columns, z_out in totals(c, total, one, 16):
            x_one = (rbuf[c % 2, :, columns].astype(F32) + z_out).astype(BF16)
            x1[c, :, columns] = x_one
            x_one = x_one.astype(F32)
            square += jnp.sum(x_one * x_one, axis=1, keepdims=True)
        inv_rms = lax.rsqrt(square / width + RMS_EPS)
        for n in range(width // 512):
            columns = pl.ds(n * 512, 512)
            done[:, columns] = (x1[c, :, columns].astype(F32) * inv_rms * gain_m_ref[:, columns]).astype(BF16)

    def finish_two(c, total, done):
        for columns, z_out in totals(c, total, two, 24):
            done[:, columns] = (x1[c, :, columns].astype(F32) + z_out).astype(BF16)

    @pl.loop(0, count + 2 * LAG)
    def _(slot):
        one.stages(slot, count, finish_one, lambda c: load_r(c).start())

        @pl.when(slot < count)
        def _():
            attention(slot)
            one.start(one.copy0(slot))

        @pl.when((slot >= LAG) & (slot < count + LAG))
        def _():
            load_h(slot - LAG).start()

        two.stages(slot - LAG, count, finish_two, lambda c: None)

        @pl.when((slot >= LAG) & (slot < count + LAG))
        def _():
            mlp(slot - LAG)
            two.start(two.copy0(slot - LAG))


def solution(mesh):
    act_spec = P('dp', None, None)
    w_head_spec = P(None, 'tp', None)
    w_out_spec = P('tp', None, None)
    w_col_spec = P(None, 'tp')
    w_row_spec = P('tp', None)
    a_rank_spec = P(None, None, 'tp')
    b_head_spec = P(None, None, 'tp', None)
    b_col_spec = P(None, None, 'tp')
    a_head_spec = P(None, 'tp', None, None)
    a_row_spec = P(None, 'tp', None)
    in_specs = (act_spec, P('dp'), P(None), P(None), w_head_spec, w_head_spec, w_head_spec, w_out_spec,
                w_col_spec, w_col_spec, w_row_spec, a_rank_spec, b_head_spec, a_rank_spec, b_head_spec,
                a_rank_spec, b_head_spec, a_head_spec, b_col_spec, a_rank_spec, b_col_spec,
                a_rank_spec, b_col_spec, a_row_spec, b_col_spec)

    def local_layer(x_in, adapter_ids, gain_attn, gain_mlp, w_q, w_k, w_v, w_o, w_gate, w_up, w_down,
                    a_q, b_q, a_k, b_k, a_v, b_v, a_o, b_o, a_gate, b_gate, a_up, b_up, a_down, b_down):
        count, seq_len, width = x_in.shape
        adapters, rank = b_q.shape[:2]
        mixed = adapters * rank
        scale = value_a10 / rank
        ff = w_gate.shape[1]

        group = mesh.shape['tp']
        head_dim = w_k.shape[2]
        n_q, n_k = w_q[0].size, w_k[0].size

        def plane(b):
            return b.transpose(1, 0, 2).reshape(group, adapters, -1)

        def planes(parts):
            zero = jnp.zeros_like(parts[0])
            return jnp.stack(list(parts) + [zero] * (4 - len(parts)), 1).reshape(4 * mixed, -1)

        a_loc = [a.transpose(2, 0, 1).reshape(adapters, width) for a in (a_q, a_k, a_v, a_gate, a_up)]
        b_loc = [b.reshape(adapters, -1) for b in (b_o, b_down)]
        own = jnp.stack([jnp.concatenate(a_loc[:3] + [jnp.zeros_like(a_loc[0])], 0),
                         jnp.concatenate(a_loc[3:] + b_loc, 0)])
        b_in = [plane(b.reshape(adapters, rank, -1)) for b in (b_q, b_k, b_v)]
        n_all = n_q + 2 * n_k
        b_qkv = planes([jnp.pad(b, ((0, 0), (0, 0), (at, n_all - at - b.shape[2])))
                        for b, at in zip(b_in, (0, n_q, n_q + n_k))])
        b_g = planes([plane(b_gate)])
        b_u = planes([jnp.zeros_like(plane(b_up)), plane(b_up)])

        index = jnp.arange(4 * mixed)
        mine = index % adapters == adapter_ids[:, None]
        index_plane = index // adapters % 4
        lane = jnp.arange(LANES)
        masks = jnp.concatenate([mine & (index_plane < 3), mine & (index_plane < 2),
                                 lane // rank == adapter_ids[:, None]], 1).astype(F32)
        amask = jnp.broadcast_to((jnp.arange(adapters) == adapter_ids[:, None])[:, :, None].astype(F32),
                                 (count, adapters, LANES))
        w_all = jnp.concatenate([w.reshape(width, -1) for w in (w_q, w_k, w_v)], 1)
        a_o_t = a_o.transpose(0, 3, 1, 2).reshape(mixed, -1)
        a_d_t = a_down.transpose(0, 2, 1).reshape(mixed, -1)

        gtile, dtile = 256, 512
        dma = pltpu.SemaphoreType.DMA
        exchange_scratch = Exchange.scratch(seq_len, width + LANES, width)
        own_rows = seq_len // 2 // CHIPS
        out, _ = pl.pallas_call(
            functools.partial(layer_kernel, count, scale, rank, n_q // head_dim, head_dim),
            out_shape=(jax.ShapeDtypeStruct(x_in.shape, BF16), jax.ShapeDtypeStruct(x_in.shape, BF16)),
            in_specs=[ANY] * 6 + [VMEM] * 10, out_specs=(ANY, ANY),
            scratch_shapes=exchange_scratch * 2 + [pltpu.VMEM((2, 4 * mixed, width), BF16)] + Gather.scratch() + [
                pltpu.VMEM((width, n_all), BF16), pltpu.VMEM((n_q, width), BF16),
                pltpu.VMEM((width // dtile, ff, dtile), BF16), pltpu.VMEM((3, width, gtile), BF16),
                pltpu.VMEM((seq_len, width), BF16), pltpu.VMEM((seq_len, n_all), BF16),
                pltpu.VMEM((seq_len, n_q), BF16), pltpu.VMEM((seq_len, ff), BF16),
                pltpu.VMEM((seq_len, 4 * mixed), BF16), pltpu.VMEM((count, own_rows, width), BF16),
                pltpu.VMEM((2, own_rows, width), BF16), dma((2,)), dma((width // dtile,)), dma((3,)), dma, dma,
                dma((2,))],
            compiler_params=pltpu.CompilerParams(collective_id=0, has_side_effects=True, vmem_limit_bytes=VMEM_LIMIT),
        )(x_in, w_all, w_o.reshape(-1, width), w_gate, w_up, w_down, own, b_qkv, b_g, b_u, a_o_t, a_d_t, masks[:, None], amask,
          gain_attn.reshape(1, -1), gain_mlp.reshape(1, -1))
        return out

    return jax.shard_map(local_layer, mesh=mesh, in_specs=in_specs, out_specs=act_spec, check_vma=False)
```

time: 492 us -> 431 us (0.88)
  matrix products: 37.1 us -> 0 us
  local copies, waits for them, and re-layouts: 57.9 us -> 24.7 us
  Pallas kernels: 368 us -> 397 us
  between operations: 13.7 us -> 0.07 us
    dot_general x4 -> x0, matrix products: 37.1 us -> none  [the longest x1 18.6 us: local_layer(): base = jnp.einsum('bsd,de->bse', h_norm, w_all, preferred_element_type=F32)]
    pallas_call x2 -> x1, Pallas kernels: 368 us -> 397 us  [local_layer(): pl.pallas_call(functools.partial(layer_kernel, count, scale, rank, n_q //...]
    slice x7 -> x0, local copies, waits for them, and re-layouts: 12.3 us -> none  [the longest x2 4.21 us: local_layer(): packed[:, n_a:].reshape(-1, 2, adapters, rank, cols)]
    reduce_sum x2 -> x0, other arithmetic: 10.2 us -> none  [the longest x1 8.31 us: rms_scale(): jnp.mean(x_f32 * x_f32, axis=-1, keepdims=True) + RMS_EPS]
    reshape x5 -> x1, local copies, waits for them, and re-layouts: 7.74 us -> 0.87 us  [local_layer(): b_in = [plane(b.reshape(adapters, rank, -1)) for b in (b_q, b_k, b_v)]]
    unnamed x22 -> x8, local copies, waits for them, and re-layouts: 22.4 us -> 18.7 us
  transfers between devices with their start and end apart: 1 -> 0, of which waited for: 0 -> 0; matrix products, arithmetic and copies ran while one was open for 9% -> 0% of each run, Pallas kernels for 0% -> 0%
where the time goes in v2:
time: 431 us; the launch traced here: 430 us
  Pallas kernels  397 us (92%)
  local copies, waits for them, and re-layouts  24.7 us (6%)
  other arithmetic  8.77 us (2%)
    pallas_call x1, Pallas kernels, local_layer(): pl.pallas_call(functools.partial(layer_kernel, count, scale, rank, n_q //...  397 us
    unnamed x8, local copies, waits for them, and re-layouts  18.7 us

profile of v2, /device:TPU:81, one launch (start us, length us, event | category | flops | bytes accessed | tf_op | source)
XLA Modules:
  0.0 430.1 jit_solution(414612080313629301)
XLA Ops:
  0.0 0.1 pad.27.clone
  0.1 0.1 pad.23.clone
  0.2 0.1 pad.37.clone
  0.2 0.8 compare_bitcast_fusion
  1.1 0.7 fusion
  1.8 0.7 fusion.2
  2.6 0.6 copy.48.masks_ref
  3.2 0.7 broadcast_in_dim.5.amask_ref
  3.9 0.9 reshape.270
  4.7 0.9 copy.50
  5.6 0.9 copy.51
  6.5 0.8 pad_bitcast_fusion
  7.2 0.1 maximum_maximum_fusion.2
  7.3 0.8 copy.45
  8.2 1.0 copy.46
  9.2 1.0 copy.47
  10.1 1.1 maximum_bitcast_fusion
  11.2 0.8 pad_maximum_fusion.1.own_ref
  12.1 1.4 maximum_maximum_fusion.1
  13.5 2.9 copy.53
  16.4 0.0 copy-done
  16.4 3.0 pad_maximum_fusion.wqkv_ref
  19.5 396.6 %shard_map.235 = (bf16[8,256,4096]{2,1,0:T(8,128)(2,1)}, bf16[8,256,4096]{2,1,0:T(8,128)(2,1)}) custom-call(bf16[8,256,4096]{2,1,0:T(8,128)(2,1)} %x_ref.1, bf16[4096,768]{1,0:T(8,128)(2,1)} %pad_maximum_fusion.wqkv_ref, bf16[512,4096]{1,0:T(8,128)(2,1)} %bitcast.58, bf16[4096,1792]{1,0:T(8,128)(2,1)} %wg_ref.1, bf16[4096,1792]{1,0:T(8,128)(2,1)} %wu_ref.1, ...), custom_call_target="tpu_custom_call" | custom-call | tf_op jit(solution)/shard_map/pallas_call | solution.py:522
  416.1 14.1 %copy.55 = bf16[8,256,4096]{2,1,0:T(8,128)(2,1)} copy(bf16[8,256,4096]{2,1,0:T(8,128)(2,1)} %get-tuple-element.6) | data formatting | bytes 33554432
  (11 shorter events, 0.1 us)
Async XLA Ops:
  0.0 16.4 %copy-start = (bf16[4096,1,128]{2,0,1:T(8,128)(2,1)S(1)}, bf16[4096,1,128]{2,0,1:T(8,128)(2,1)}, u32[]{:S(2)}) copy-start(bf16[4096,1,128]{2,0,1:T(8,128)(2,1)} %param.31) | copy-start | bytes 3145732
  0.0 16.4 %copy-start.1 = (bf16[4096,1,128]{2,0,1:T(8,128)(2,1)S(1)}, bf16[4096,1,128]{2,0,1:T(8,128)(2,1)}, u32[]{:S(2)}) copy-start(bf16[4096,1,128]{2,0,1:T(8,128)(2,1)} %param.30) | copy-start | bytes 3145732

commit v3 on v2

--- a/solution.py
+++ b/solution.py
@@ -17,7 +17,7 @@
 VMEM_LIMIT = 67043328
 LANES = 128
 CHIPS = 4
-LAG = 6
+LAG = 3
 
 
 class Exchange:
@@ -45,7 +45,7 @@
         dma = pltpu.SemaphoreType.DMA
         return [pltpu.VMEM((seq_len, width), BF16), pltpu.VMEM((2, half, width), BF16),
                 pltpu.VMEM((2, 2, rows // 2, width), BF16), pltpu.VMEM((2, 2, rows, width), BF16),
-                pltpu.VMEM((3, half, width), BF16), pltpu.VMEM((2, rows, done_width), BF16),
+                pltpu.VMEM((2, half, width), BF16), pltpu.VMEM((2, rows, done_width), BF16),
                 dma((2,)), dma((2,)), dma((2, 2)), dma((2, 2)), dma((2, 2)), dma((2, 2)),
                 dma((3, 2)), dma((3, 2)), dma((4, 2)), dma((4, 2)), dma((2,)), dma((2,)), dma((2,))]
 
@@ -71,7 +71,7 @@
                           self.r0.at[c % 2], self.partner)]
 
     def copy1(self, c):
-        quart, far = self.quart.at[c % 3], self.slab(2)
+        quart, far = self.quart.at[c % 2], self.slab(2)
         low = pl.multiple_of(far + self.hrows, self.hrows)
         return [self.send(quart.at[pl.ds(far, self.hrows)], self.recv1.at[0, c % 2], self.s1.at[0, c % 2],
                           self.r1.at[0, c % 2], self.right),
@@ -79,7 +79,7 @@
                           self.r1.at[1, c % 2], self.left)]
 
     def copy2(self, c):
-        quart = self.quart.at[c % 3]
+        quart = self.quart.at[c % 2]
         return [self.send(quart.at[pl.ds(self.slab(1), self.rows)], self.recv2.at[0, c % 2], self.s2.at[0, c % 2],
                           self.r2.at[0, c % 2], self.right),
                 self.send(quart.at[pl.ds(self.slab(CHIPS - 1), self.rows)], self.recv2.at[1, c % 2],
@@ -128,7 +128,7 @@
     def add_pair(self, c):
         self.wait_recv(self.copy0(c))
         self.wait_send(self.copy0(c))
-        quart, recv = self.quart.at[c % 3], self.recv0.at[c % 2]
+        quart, recv = self.quart.at[c % 2], self.recv0.at[c % 2]
         own = self.core * self.half
 
         @pl.loop(0, self.half // 16)
@@ -141,7 +141,7 @@
 
     def add_far(self, c):
         self.wait_recv(self.copy1(c))
-        quart = self.quart.at[c % 3]
+        quart = self.quart.at[c % 2]
         for side, first in ((0, self.slab(1)), (1, self.slab(CHIPS - 1) + self.hrows)):
             rows = pl.ds(pl.multiple_of(first, self.hrows), self.hrows)
             quart[rows, :] = (quart[rows, :].astype(F32) + self.recv1[side, c % 2].astype(F32)).astype(BF16)
@@ -150,7 +150,7 @@
     def finish(self, c, finalize):
         self.wait_recv(self.copy2(c))
         self.wait_send(self.copy1(c))
-        quart, slot = self.quart.at[c % 3], c % 2
+        quart, slot = self.quart.at[c % 2], c % 2
 
         def total(first, size, columns):
             rows = pl.ds(pl.multiple_of(self.slab(0) + first, size), size)
@@ -178,13 +178,18 @@
         self.wait_send(self.copy_b(c))
         self.wait_send(self.copy_c(c))
 
-    def stages(self, slot, count, finalize, prefetch):
+    def first_stages(self, slot, count, finalize):
+        self.run(slot, count, ((2, self.cross), (1, lambda c: self.finish(c, finalize)), (0, self.add_pair)))
+
+    def second_stages(self, slot, count, prefetch):
         def far(c):
             prefetch(c)
             self.add_far(c)
 
-        table = ((6, self.close), (5, self.cross), (4, self.forward),
-                 (3, lambda c: self.finish(c, finalize)), (2, far), (1, self.add_pair))
+        self.run(slot, count, ((3, self.close), (2, self.forward), (1, far)))
+
+    @staticmethod
+    def run(slot, count, table):
         for lag, stage in table:
             @pl.when((slot >= lag) & (slot < count + lag))
             def _(lag=lag, stage=stage):
@@ -264,6 +269,7 @@
     seq_len, width = ubuf.shape
     gtile, dtile = ring.shape[2], wd.shape[2]
     pairs, downs = mid.shape[1] // gtile, wd.shape[0]
+    otile = 1024
     mixed = full.shape[1]
 
     def load_x(c):
@@ -301,12 +307,17 @@
     def attention(c):
         load_x(c).wait()
 
-        @pl.loop(0, seq_len // 16)
+        @pl.loop(0, seq_len // 64)
         def _(i):
-            rows = pl.ds(pl.multiple_of(i * 16, 16), 16)
-            value = ubuf[rows, :].astype(F32)
-            inv_rms = lax.rsqrt(jnp.sum(value * value, axis=1, keepdims=True) / width + RMS_EPS)
-            ubuf[rows, :] = (value * inv_rms * gain_a_ref[...]).astype(BF16)
+            rows = pl.ds(pl.multiple_of(i * 64, 64), 64)
+            square = jnp.zeros((64, LANES), F32)
+            for n in range(width // LANES):
+                value = ubuf[rows, n * LANES:(n + 1) * LANES].astype(F32)
+                square += value * value
+            inv_rms = lax.rsqrt(jnp.sum(square, axis=1, keepdims=True) / width + RMS_EPS)
+            for n in range(width // LANES):
+                columns = pl.ds(n * LANES, LANES)
+                ubuf[rows, columns] = (ubuf[rows, columns].astype(F32) * inv_rms * gain_a_ref[:, columns]).astype(BF16)
 
         @pl.when(c == 0)
         def _():
@@ -318,11 +329,7 @@
 
         @pl.when(c == 1)
         def _():
-            gather.forward(1)
-
-        @pl.when(c == 2)
-        def _():
-            gather.cross(1)
+            gather.close(1)
 
         keep = masks_ref[c, :, 0:mixed] > 0
         t_buf[...] = jnp.where(keep, dot_t(ubuf[...], full[0]).astype(BF16).astype(F32), 0.0).astype(BF16)
@@ -333,9 +340,17 @@
             base = dot(ubuf[...], wqkv[:, columns])
             qkv[:, columns] = (base + scale * dot(t_buf[...], bqkv_ref[:, columns])).astype(BF16)
 
+        @pl.when(c >= LAG)
+        def _():
+            load_h(c - LAG).start()
+
         @pl.when((c + 1 < count) & (c < LAG))
         def _():
             load_x(c + 1).start()
+
+        @pl.when(c == 0)
+        def _():
+            gather.forward(1)
 
         kv_heads = (qkv.shape[1] // head_dim - heads) // 2
         causal = (lax.broadcasted_iota(jnp.int32, (seq_len, seq_len), 0)
@@ -348,23 +363,24 @@
             prob = (prob / jnp.sum(prob, axis=1, keepdims=True)).astype(BF16)
             att[:, j * head_dim:(j + 1) * head_dim] = dot(prob, value).astype(BF16)
 
-        @pl.loop(0, width // 512)
+        @pl.loop(0, width // otile)
         def _(n):
-            columns = pl.ds(pl.multiple_of(n * 512, 512), 512)
+            columns = pl.ds(pl.multiple_of(n * otile, otile), otile)
             one.part[:, columns] = dot(att[...], wo[:, columns]).astype(BF16)
 
         pad = jnp.zeros((seq_len, LANES - ao_ref.shape[0]), F32)
         one.part[:, width:] = jnp.concatenate([dot_t(att[...], ao_ref[...]), pad], 1).astype(BF16)
 
-        @pl.when(c == 2)
-        def _():
-            gather.close(1)
-
-    def mlp(c):
+        @pl.when(c == 0)
+        def _():
+            gather.cross(1)
+
+    def mlp_start(c):
         load_h(c).wait()
         keep = masks_ref[c, :, mixed:2 * mixed] > 0
         t_buf[...] = jnp.where(keep, dot_t(ubuf[...], full[1]).astype(BF16).astype(F32), 0.0).astype(BF16)
 
+    def gate_up(c, begin, end):
         def product(w_ref, b_ref, j, side):
             copy, place = load_tile(w_ref, c, j, side)
             copy.wait()
@@ -378,7 +394,7 @@
             def _():
                 load_tile(w_ref, c + wrap, j % pairs, side)[0].start()
 
-        @pl.loop(0, pairs)
+        @pl.loop(begin, end)
         def _(j):
             columns = pl.ds(pl.multiple_of(j * gtile, gtile), gtile)
             mid[:, columns] = product(wg_ref, bg_ref, j, 0)
@@ -387,6 +403,7 @@
             refill(wg_ref, j + 2, 0)
             mid[:, columns] = (jax.nn.silu(mid[:, columns].astype(F32)) * up.astype(F32)).astype(BF16)
 
+    def down(c):
         @pl.when(c + LAG + 1 < count)
         def _():
             load_x(c + LAG + 1).start()
@@ -436,25 +453,38 @@
         for columns, z_out in totals(c, total, two, 24):
             done[:, columns] = (x1[c, :, columns].astype(F32) + z_out).astype(BF16)
 
+    split = pairs // 2
+
     @pl.loop(0, count + 2 * LAG)
     def _(slot):
-        one.stages(slot, count, finish_one, lambda c: load_r(c).start())
+        late = slot - LAG
+        busy = (slot >= LAG) & (slot < count + LAG)
+        one.second_stages(slot, count, lambda c: load_r(c).start())
+
+        @pl.when((slot >= count) & busy)
+        def _():
+            load_h(late).start()
+
+        two.first_stages(late - 1, count, finish_two)
 
         @pl.when(slot < count)
         def _():
             attention(slot)
             one.start(one.copy0(slot))
 
-        @pl.when((slot >= LAG) & (slot < count + LAG))
-        def _():
-            load_h(slot - LAG).start()
-
-        two.stages(slot - LAG, count, finish_two, lambda c: None)
-
-        @pl.when((slot >= LAG) & (slot < count + LAG))
-        def _():
-            mlp(slot - LAG)
-            two.start(two.copy0(slot - LAG))
+        @pl.when(busy)
+        def _():
+            mlp_start(late)
+            gate_up(late, 0, split)
+
+        one.first_stages(slot, count, finish_one)
+        two.second_stages(late, count, lambda c: None)
+
+        @pl.when(busy)
+        def _():
+            gate_up(late, split, pairs)
+            down(late)
+            two.start(two.copy0(late))
 
 
 def solution(mesh):
@@ -515,7 +545,7 @@
         a_o_t = a_o.transpose(0, 3, 1, 2).reshape(mixed, -1)
         a_d_t = a_down.transpose(0, 2, 1).reshape(mixed, -1)
 
-        gtile, dtile = 256, 512
+        gtile, dtile = 256, 1024
         dma = pltpu.SemaphoreType.DMA
         exchange_scratch = Exchange.scratch(seq_len, width + LANES, width)
         own_rows = seq_len // 2 // CHIPS

time: 431 us -> 420 us (0.974)
  Pallas kernels: 397 us -> 386 us
    pallas_call x1, Pallas kernels: 397 us -> 386 us  [local_layer(): pl.pallas_call(functools.partial(layer_kernel, count, scale, rank, n_q //...]
where the time goes in v3:
time: 420 us
  Pallas kernels  386 us (92%)
  local copies, waits for them, and re-layouts  24.7 us (6%)
  other arithmetic  8.77 us (2%)
    pallas_call x1, Pallas kernels, local_layer(): pl.pallas_call(functools.partial(layer_kernel, count, scale, rank, n_q //...  386 us
    unnamed x8, local copies, waits for them, and re-layouts  18.7 us

profile of v3, /device:TPU:81, one launch (start us, length us, event | category | flops | bytes accessed | tf_op | source)
XLA Modules:
  0.0 419.8 jit_solution(8244062224101975768)
XLA Ops:
  0.0 0.1 pad.27.clone
  0.1 0.1 pad.23.clone
  0.2 0.1 pad.37.clone
  0.2 0.8 compare_bitcast_fusion
  1.1 0.7 fusion
  1.8 0.7 fusion.2
  2.6 0.6 copy.48.masks_ref
  3.2 0.7 broadcast_in_dim.5.amask_ref
  3.9 0.9 reshape.270
  4.7 0.9 copy.50
  5.6 0.9 copy.51
  6.5 0.8 pad_bitcast_fusion
  7.2 0.1 maximum_maximum_fusion.2
  7.3 0.8 copy.45
  8.2 1.0 copy.46
  9.2 1.0 copy.47
  10.1 1.1 maximum_bitcast_fusion
  11.2 0.8 pad_maximum_fusion.1.own_ref
  12.1 1.4 maximum_maximum_fusion.1
  13.5 2.9 copy.53
  16.4 0.0 copy-done
  16.4 3.0 pad_maximum_fusion.wqkv_ref
  19.5 386.3 %shard_map.235 = (bf16[8,256,4096]{2,1,0:T(8,128)(2,1)}, bf16[8,256,4096]{2,1,0:T(8,128)(2,1)}) custom-call(bf16[8,256,4096]{2,1,0:T(8,128)(2,1)} %x_ref.1, bf16[4096,768]{1,0:T(8,128)(2,1)} %pad_maximum_fusion.wqkv_ref, bf16[512,4096]{1,0:T(8,128)(2,1)} %bitcast.58, bf16[4096,1792]{1,0:T(8,128)(2,1)} %wg_ref.1, bf16[4096,1792]{1,0:T(8,128)(2,1)} %wu_ref.1, ...), custom_call_target="tpu_custom_call" | custom-call | tf_op jit(solution)/shard_map/pallas_call | solution.py:552
  405.8 14.1 %copy.55 = bf16[8,256,4096]{2,1,0:T(8,128)(2,1)} copy(bf16[8,256,4096]{2,1,0:T(8,128)(2,1)} %get-tuple-element.6) | data formatting | bytes 33554432
  (11 shorter events, 0.1 us)
Async XLA Ops:
  0.0 16.4 %copy-start = (bf16[4096,1,128]{2,0,1:T(8,128)(2,1)S(1)}, bf16[4096,1,128]{2,0,1:T(8,128)(2,1)}, u32[]{:S(2)}) copy-start(bf16[4096,1,128]{2,0,1:T(8,128)(2,1)} %param.31) | copy-start | bytes 3145732
  0.0 16.4 %copy-start.1 = (bf16[4096,1,128]{2,0,1:T(8,128)(2,1)S(1)}, bf16[4096,1,128]{2,0,1:T(8,128)(2,1)}, u32[]{:S(2)}) copy-start(bf16[4096,1,128]{2,0,1:T(8,128)(2,1)} %param.30) | copy-start | bytes 3145732

commit v4 on v3

--- a/solution.py
+++ b/solution.py
@@ -299,10 +299,6 @@
     one.barrier()
     gather.begin(0)
     gather.begin(1)
-    for w_ref, j, side in ((wg_ref, 0, 0), (wu_ref, 0, 1), (wg_ref, 1, 0)):
-        load_tile(w_ref, 0, j, side)[0].start()
-    for n in range(downs):
-        load_d(n).start()
 
     def attention(c):
         load_x(c).wait()
@@ -324,7 +320,6 @@
             gather.forward(0)
             gather.cross(0)
             load_qkv.wait()
-            load_o.wait()
             gather.close(0)
 
         @pl.when(c == 1)
@@ -351,6 +346,11 @@
         @pl.when(c == 0)
         def _():
             gather.forward(1)
+            load_o.wait()
+            for w_ref, j, side in ((wg_ref, 0, 0), (wu_ref, 0, 1), (wg_ref, 1, 0)):
+                load_tile(w_ref, 0, j, side)[0].start()
+            for n in range(downs):
+                load_d(n).start()
 
         kv_heads = (qkv.shape[1] // head_dim - heads) // 2
         causal = (lax.broadcasted_iota(jnp.int32, (seq_len, seq_len), 0)
@@ -465,24 +465,28 @@
         def _():
             load_h(late).start()
 
-        two.first_stages(late - 1, count, finish_two)
-
         @pl.when(slot < count)
         def _():
             attention(slot)
             one.start(one.copy0(slot))
 
+        two.first_stages(late - 1, count, finish_two)
+
         @pl.when(busy)
         def _():
             mlp_start(late)
             gate_up(late, 0, split)
 
         one.first_stages(slot, count, finish_one)
+
+        @pl.when(busy)
+        def _():
+            gate_up(late, split, pairs)
+
         two.second_stages(late, count, lambda c: None)
 
         @pl.when(busy)
         def _():
-            gate_up(late, split, pairs)
             down(late)
             two.start(two.copy0(late))
 

time: 420 us -> 416 us (level)
    pallas_call x1, Pallas kernels: 386 us -> 382 us  [local_layer(): pl.pallas_call(functools.partial(layer_kernel, count, scale, rank, n_q //...]
where the time goes in v4:
time: 416 us; the launch traced here: 415 us
  Pallas kernels  382 us (92%)
  local copies, waits for them, and re-layouts  24.7 us (6%)
  other arithmetic  8.77 us (2%)
    pallas_call x1, Pallas kernels, local_layer(): pl.pallas_call(functools.partial(layer_kernel, count, scale, rank, n_q //...  382 us
    unnamed x8, local copies, waits for them, and re-layouts  18.7 us

profile of v4, /device:TPU:81, one launch (start us, length us, event | category | flops | bytes accessed | tf_op | source)
XLA Modules:
  0.0 415.3 jit_solution(16959403226962983718)
XLA Ops:
  0.0 0.1 pad.27.clone
  0.1 0.1 pad.23.clone
  0.2 0.1 pad.37.clone
  0.2 0.8 compare_bitcast_fusion
  1.1 0.7 fusion
  1.8 0.7 fusion.2
  2.6 0.6 copy.48.masks_ref
  3.2 0.7 broadcast_in_dim.5.amask_ref
  3.9 0.9 reshape.270
  4.7 0.9 copy.50
  5.6 0.9 copy.51
  6.5 0.8 pad_bitcast_fusion
  7.2 0.1 maximum_maximum_fusion.2
  7.3 0.8 copy.45
  8.2 1.0 copy.46
  9.2 1.0 copy.47
  10.1 1.1 maximum_bitcast_fusion
  11.2 0.8 pad_maximum_fusion.1.own_ref
  12.1 1.4 maximum_maximum_fusion.1
  13.5 2.9 copy.53
  16.4 0.0 copy-done
  16.4 3.0 pad_maximum_fusion.wqkv_ref
  19.5 381.8 %shard_map.235 = (bf16[8,256,4096]{2,1,0:T(8,128)(2,1)}, bf16[8,256,4096]{2,1,0:T(8,128)(2,1)}) custom-call(bf16[8,256,4096]{2,1,0:T(8,128)(2,1)} %x_ref.1, bf16[4096,768]{1,0:T(8,128)(2,1)} %pad_maximum_fusion.wqkv_ref, bf16[512,4096]{1,0:T(8,128)(2,1)} %bitcast.58, bf16[4096,1792]{1,0:T(8,128)(2,1)} %wg_ref.1, bf16[4096,1792]{1,0:T(8,128)(2,1)} %wu_ref.1, ...), custom_call_target="tpu_custom_call" | custom-call | tf_op jit(solution)/shard_map/pallas_call | solution.py:556
  401.2 14.1 %copy.55 = bf16[8,256,4096]{2,1,0:T(8,128)(2,1)} copy(bf16[8,256,4096]{2,1,0:T(8,128)(2,1)} %get-tuple-element.6) | data formatting | bytes 33554432
  (11 shorter events, 0.1 us)
Async XLA Ops:
  0.0 16.4 %copy-start = (bf16[4096,1,128]{2,0,1:T(8,128)(2,1)S(1)}, bf16[4096,1,128]{2,0,1:T(8,128)(2,1)}, u32[]{:S(2)}) copy-start(bf16[4096,1,128]{2,0,1:T(8,128)(2,1)} %param.31) | copy-start | bytes 3145732
  0.0 16.4 %copy-start.1 = (bf16[4096,1,128]{2,0,1:T(8,128)(2,1)S(1)}, bf16[4096,1,128]{2,0,1:T(8,128)(2,1)}, u32[]{:S(2)}) copy-start(bf16[4096,1,128]{2,0,1:T(8,128)(2,1)} %param.30) | copy-start | bytes 3145732
